TPU v7x, 128 devices: a whole 4x4x4 slice. The times are simulated.
128 devices in a mesh: gx: 16 (over y_hi, z, core), gy: 8 (over y_lo, x).
Axes of the slice: x: 4, y: 4 (y_hi: 2, y_lo: 2; y = y_hi * 2 + y_lo), z: 4, core: 2. Of those that a mesh axis runs over, the one named last changes fastest.
Arguments:
- terminal: float32 [4096, 4096], P('gx', 'gy'), may hold values from -6 to 6
- crowding: float32 [4096, 4096], P('gx', 'gy'), may hold values from 0.5 to 4
- density: float32 [4096, 4096], P('gx', 'gy'), may hold values from 0.25 to 36, as said below
- fractions: float32 [4, 2, 4096, 4096], P(None, None, 'gx', 'gy'), may hold values from 0 to 1
- offsets: int32 [4, 8, 2], replicated, may hold values from -64 to 63
- control_cost: float32 [4, 8], replicated, may hold values from 0 to 4
Outputs:
- value_start: float32 [4096, 4096], P('gx', 'gy')
- density_end: float32 [4096, 4096], P('gx', 'gy')
- masses: float32 [4], replicated
Inputs may be any that keep to these rules, and one draw needn't show every extreme that they name: `density`: positive.
All inputs are finite; a program needn't handle non-finite values.
Results may differ from a plain program's by a relative error of at most 0.0001.
Values sent between devices are 32-bit elements; how exact they have to be, the bound alone decides.
A program may use at most 128 MiB of HBM per device.

v0:
```python
from functools import reduce

import jax
import jax.numpy as jnp
from jax import lax
from jax.sharding import Mesh
from jax.sharding import PartitionSpec as P

REACH = 64
GX = ("gx_0", "gx_1", "gx_2")
GY = ("gy_0", "gy_1")
GX_GY = ("gx_0", "gx_1", "gx_2", "gy_0", "gy_1")


time_step = 0.1
temper = 0.3
epsilon = 1e-06


def with_halo(cells, sides, width):
    for axis, dim in sides:
        count = lax.axis_size(axis)
        head = lax.slice_in_dim(cells, 0, width, axis=dim)
        tail = lax.slice_in_dim(cells, cells.shape[dim] - width, cells.shape[dim], axis=dim)
        cells = jnp.concatenate(
            [
                lax.ppermute(tail, axis, [(i, (i + 1) % count) for i in range(count)]),
                cells,
                lax.ppermute(head, axis, [((i + 1) % count, i) for i in range(count)]),
            ],
            axis=dim,
        )
    return cells


def by_axis(x, axes):
    for axis in axes:
        x = lax.psum(x, axis)
    return x


def catmull(fraction):
    square = fraction * fraction
    cube = square * fraction
    return [
        (-cube + 2.0 * square - fraction) * 0.5,
        (3.0 * cube - 5.0 * square + 2.0) * 0.5,
        (-3.0 * cube + 4.0 * square + fraction) * 0.5,
        (cube - square) * 0.5,
    ]


def sample(padded, weights_x, weights_y, shift_row, shift_col, margin, height, breadth):
    summed = None
    for row_tap in range(4):
        partial_sum = None
        for col_tap in range(4):
            piece = lax.dynamic_slice(
                padded,
                (margin + shift_row + row_tap - 1, margin + shift_col + col_tap - 1),
                (height, breadth),
            )
            term = weights_y[col_tap] * piece
            partial_sum = term if partial_sum is None else partial_sum + term
        term = weights_x[row_tap] * partial_sum
        summed = term if summed is None else summed + term
    return summed


def option_values(
    padded, weights_x, weights_y, offsets, control_cost, crowding, moment, margin, height, breadth
):
    candidates = []
    for option in range(offsets.shape[1]):
        shifted = sample(
            padded,
            weights_x,
            weights_y,
            offsets[moment, option, 0],
            offsets[moment, option, 1],
            margin,
            height,
            breadth,
        )
        candidates.append(shifted + time_step * (control_cost[moment, option] + crowding))
    return candidates


def policy(candidates):
    lowest = reduce(jnp.minimum, candidates)
    ramps = [jnp.maximum(lowest + temper - candidate, 0.0) for candidate in candidates]
    ramp_sum = reduce(jnp.add, ramps)
    return (lowest, [ramp / ramp_sum for ramp in ramps])


def shards(terminal, crowding, density, fractions, offsets, control_cost):
    margin = REACH + 2
    height, breadth = terminal.shape
    steps_count = fractions.shape[0]
    controls_count = offsets.shape[1]
    cells = height * breadth * lax.axis_size(GX) * lax.axis_size(GY)
    current_value = terminal
    policies = [None] * steps_count
    stored = [None] * steps_count
    for moment in reversed(range(steps_count)):
        padded = with_halo(current_value, ((GX, 0), (GY, 1)), margin)
        weights_x = catmull(fractions[moment, 0])
        weights_y = catmull(fractions[moment, 1])
        candidates = option_values(
            padded,
            weights_x,
            weights_y,
            offsets,
            control_cost,
            crowding,
            moment,
            margin,
            height,
            breadth,
        )
        stored[moment] = current_value
        current_value, policies[moment] = policy(candidates)
    current = density
    local_sums = []
    for moment in range(steps_count):
        weights_x = catmull(fractions[moment, 0])
        weights_y = catmull(fractions[moment, 1])
        weights_now = policies[moment]
        padded = with_halo(current, ((GX, 0), (GY, 1)), margin)
        arrived = None
        for option in range(controls_count):
            shifted = sample(
                padded,
                weights_x,
                weights_y,
                -offsets[moment, option, 0],
                -offsets[moment, option, 1],
                margin,
                height,
                breadth,
            )
            term = weights_now[option] * shifted
            arrived = term if arrived is None else arrived + term
        arrived = jnp.maximum(arrived, 0.0)
        local_sums.append(jnp.sum(arrived))
        current = arrived
    totals = by_axis(jnp.stack(local_sums), GX_GY) / cells
    masses = jnp.concatenate([totals[:1], totals[1:] / totals[:-1]])
    current = current / (totals[-1] + epsilon)
    return (current_value, current, masses)


def solution(mesh):
    finer = Mesh(mesh.devices.reshape(2, 4, 2, 2, 4), ("gx_0", "gx_1", "gx_2", "gy_0", "gy_1"))
    placed = (P(GX, GY), P(GX, GY), P(GX, GY), P(None, None, GX, GY), P(), P())
    return jax.shard_map(
        shards, mesh=finer, in_specs=placed, out_specs=(P(GX, GY), P(GX, GY), P()), check_vma=False
    )
```

profile of v0, /device:TPU:1, one launch (start us, length us, event | category | flops | bytes accessed | tf_op | source)
XLA Modules:
  0.0 831.3 jit_solution(342333851067521364)
XLA Ops:
  93.4 30.9 %minimum_minimum_fusion.5 = (f32[256,512]{1,0:T(8,128)S(1)}, f32[256,512]{1,0:T(8,128)}, f32[256,512]{1,0:T(8,128)}, f32[256,512]{1,0:T(8,128)}, f32[256,512]{1,...) fusion(f32[256,512]{1,0:T(8,128)S(1)} %copy-done, ...), kind=kLoop, calls=%fused_computation.186 | loop fusion | flops 45744128 | bytes 73400608 | tf_op jit(solution)/shard_map/min | solution.py:90
  124.3 4.4 collective-permute-start.4
  219.2 31.0 %minimum_minimum_fusion.3 = (f32[256,512]{1,0:T(8,128)S(1)}, f32[256,512]{1,0:T(8,128)}, f32[256,512]{1,0:T(8,128)}, f32[256,512]{1,0:T(8,128)}, f32[256,512]{1,...) fusion(f32[256,512]{1,0:T(8,128)S(1)} %copy-done, ...), kind=kLoop, calls=%fused_computation.176 | loop fusion | flops 45744128 | bytes 73400608 | tf_op jit(solution)/shard_map/min | solution.py:90
  252.5 4.0 collective-permute-start.9
  257.3 5.3 collective-permute-start.17
  313.3 4.0 collective-permute-start.11
  438.5 31.3 %minimum_minimum_fusion.1 = (f32[256,512]{1,0:T(8,128)S(1)}, f32[256,512]{1,0:T(8,128)}, f32[256,512]{1,0:T(8,128)}, f32[256,512]{1,0:T(8,128)}, f32[256,512]{1,...) fusion(f32[256,512]{1,0:T(8,128)S(1)} %copy-done, ...), kind=kLoop, calls=%fused_computation.166 | loop fusion | flops 45744128 | bytes 73400608 | tf_op jit(solution)/shard_map/min | solution.py:90
  469.9 5.7 collective-permute-start.13
  475.8 3.6 collective-permute-start.19
  479.6 3.7 collective-permute-start.15
  488.2 145.9 %fusion.104 = (f32[]{:T(128)}, f32[256,512]{1,0:T(8,128)S(1)}, f32[256,512]{1,0:T(8,128)}) fusion(f32[388,644]{1,0:T(8,128)S(1)} %pad_maximum_fusion.4, s32[]{:T(128)S(6)} %select_n.1343, s32[]{:T(128)S(6)} %select_n.1340, s32[]{:T(128)S(6)} %select_n.1339, s32[]{:T(128)S(6)} %select_n.1338, s32[]{:T(128)S(6)} %select_n.1337, s32[]{:T(128)S(6)} %select_n.1342, ...), kind=kLoop, calls=%fused_computation.224 | loop fusion | flops 88866816 | bytes 136839712 | tf_op jit(solution)/shard_map/reduce_sum | solution.py:145
  634.2 9.2 %collective-permute-start.21 = (f32[66,512]{1,0:T(8,128)S(1)}, f32[66,512]{1,0:T(8,128)S(1)}, u32[]{:S(2)}, u32[]{:S(2)}) collective-permute-start(f32[66,512]{1,0:T(8,128)S(1)} %get-tuple-element.60), channel_id=1, source_target_pairs={{8,0},{16,8},{24,16},{32,24},{40,32},{48,40},{56,48},{64,56},{72,6... | collective-permute-start | bytes 405512 | tf_op jit(solution)/shard_map/ppermute | solution.py:29
  645.2 4.0 collective-permute-start.23
  661.5 25.9 %fusion.105 = (f32[]{:T(128)}, f32[256,512]{1,0:T(8,128)S(1)}) fusion(f32[388,644]{1,0:T(8,128)S(1)} %pad_maximum_fusion.5, s32[]{:T(128)S(6)} %select_n.1407, s32[]{:T(128)S(6)} %select_n.1404, s32[]{:T(128)S(6)} %select_n.1403, s32[]{:T(128)S(6)} %select_n.1402, s32[]{:T(128)S(6)} %select_n.1401, s32[]{:T(128)S(6)} %select_n.1406, s32[]{:T(128)S(6)} %select_n.1405, ...), kind=kLoop, calls=%fused_computation.225 | loop fusion | flops 49020928 | bytes 72876288 | tf_op jit(solution)/shard_map/reduce_sum | solution.py:145
  687.6 7.7 collective-permute-start.25
  697.1 3.6 collective-permute-start.27
  713.0 25.7 %fusion.106 = (f32[]{:T(128)}, f32[256,512]{1,0:T(8,128)S(1)}) fusion(f32[388,644]{1,0:T(8,128)S(1)} %pad_maximum_fusion.6, s32[]{:T(128)S(6)} %select_n.1471, s32[]{:T(128)S(6)} %select_n.1468, s32[]{:T(128)S(6)} %select_n.1467, s32[]{:T(128)S(6)} %select_n.1466, s32[]{:T(128)S(6)} %select_n.1465, s32[]{:T(128)S(6)} %select_n.1470, s32[]{:T(128)S(6)} %select_n.1469, ...), kind=kLoop, calls=%fused_computation.226 | loop fusion | flops 49020928 | bytes 72876288 | tf_op jit(solution)/shard_map/reduce_sum | solution.py:145
  738.7 8.0 collective-permute-start.29
  748.5 3.8 collective-permute-start.31
  764.3 26.0 %fusion.107 = (f32[]{:T(128)}, f32[256,512]{1,0:T(8,128)S(1)}) fusion(f32[388,644]{1,0:T(8,128)S(1)} %pad_maximum_fusion.7, s32[]{:T(128)S(6)} %select_n.1535, s32[]{:T(128)S(6)} %select_n.1532, s32[]{:T(128)S(6)} %select_n.1531, s32[]{:T(128)S(6)} %select_n.1530, s32[]{:T(128)S(6)} %select_n.1529, s32[]{:T(128)S(6)} %select_n.1534, s32[]{:T(128)S(6)} %select_n.1533, ...), kind=kLoop, calls=%fused_computation.227 | loop fusion | flops 49020928 | bytes 72876288 | tf_op jit(solution)/shard_map/reduce_sum | solution.py:145
  793.0 5.3 psum.35
  798.2 15.3 %psum.36 = f32[4]{0:T(128)S(1)} all-reduce(f32[4]{0:T(128)S(1)} %psum.35), channel_id=1, replica_groups=mesh['gx_0'=2,'gx_1'=4,'gx_2'=2,'gy_0'=2,'gy_1'=4] {'gx_1'}, use_global_device_ids=true, to_apply=%region_5.0 | all-reduce | flops 4 | bytes 32 | tf_op jit(solution)/shard_map/psum | solution.py:38
  816.9 3.9 psum.38
  820.8 6.6 psum.39
  (148 shorter events, 54.4 us)
Async XLA Ops:
  1.7 84.3 %collective-permute-start = (f32[66,512]{1,0:T(8,128)S(1)}, f32[66,512]{1,0:T(8,128)S(1)}, u32[]{:S(2)}, u32[]{:S(2)}) collective-permute-start(f32[66,512]{1,0:T(8,128)S(1)} %get-tuple-element.67), channel_id=1, source_target_pairs={{0,8},{8,16},{16,24},{24,32},{32,40},{40,48},{48,56},{56,64},{64,7... | collective-permute-start | bytes 405512 | tf_op jit(solution)/shard_map/ppermute | solution.py:27
  4.8 81.2 %collective-permute-start.1 = (f32[66,512]{1,0:T(8,128)S(1)}, f32[66,512]{1,0:T(8,128)S(1)}, u32[]{:S(2)}, u32[]{:S(2)}) collective-permute-start(f32[66,512]{1,0:T(8,128)S(1)} %get-tuple-element.68), channel_id=1, source_target_pairs={{8,0},{16,8},{24,16},{32,24},{40,32},{48,40},{56,48},{64,56},{72,6... | collective-permute-start | bytes 405512 | tf_op jit(solution)/shard_map/ppermute | solution.py:29
  124.3 87.1 %collective-permute-start.4 = (f32[66,512]{1,0:T(8,128)S(1)}, f32[66,512]{1,0:T(8,128)S(1)}, u32[]{:S(2)}, u32[]{:S(2)}) collective-permute-start(f32[66,512]{1,0:T(8,128)S(1)} %get-tuple-element.65), channel_id=1, source_target_pairs={{0,8},{8,16},{16,24},{24,32},{32,40},{40,48},{48,56},{56,64},{64,7... | collective-permute-start | bytes 405512 | tf_op jit(solution)/shard_map/ppermute | solution.py:27
  128.7 82.7 %collective-permute-start.5 = (f32[66,512]{1,0:T(8,128)S(1)}, f32[66,512]{1,0:T(8,128)S(1)}, u32[]{:S(2)}, u32[]{:S(2)}) collective-permute-start(f32[66,512]{1,0:T(8,128)S(1)} %get-tuple-element.66), channel_id=1, source_target_pairs={{8,0},{16,8},{24,16},{32,24},{40,32},{48,40},{56,48},{64,56},{72,6... | collective-permute-start | bytes 405512 | tf_op jit(solution)/shard_map/ppermute | solution.py:29
  250.2 62.5 %collective-permute-start.8 = (f32[66,512]{1,0:T(8,128)S(1)}, f32[66,512]{1,0:T(8,128)S(1)}, u32[]{:S(2)}, u32[]{:S(2)}) collective-permute-start(f32[66,512]{1,0:T(8,128)S(1)} %get-tuple-element.63), channel_id=1, source_target_pairs={{0,8},{8,16},{16,24},{24,32},{32,40},{40,48},{48,56},{56,64},{64,7... | collective-permute-start | bytes 405512 | tf_op jit(solution)/shard_map/ppermute | solution.py:27
  252.5 60.2 %collective-permute-start.9 = (f32[66,512]{1,0:T(8,128)S(1)}, f32[66,512]{1,0:T(8,128)S(1)}, u32[]{:S(2)}, u32[]{:S(2)}) collective-permute-start(f32[66,512]{1,0:T(8,128)S(1)} %get-tuple-element.64), channel_id=1, source_target_pairs={{8,0},{16,8},{24,16},{32,24},{40,32},{48,40},{56,48},{64,56},{72,6... | collective-permute-start | bytes 405512 | tf_op jit(solution)/shard_map/ppermute | solution.py:29
  257.2 218.4 %collective-permute-start.16 = (f32[66,512]{1,0:T(8,128)}, f32[66,512]{1,0:T(8,128)S(1)}, u32[]{:S(2)}, u32[]{:S(2)}) collective-permute-start(f32[66,512]{1,0:T(8,128)} %get-tuple-element.69), channel_id=1, source_target_pairs={{0,8},{8,16},{16,24},{24,32},{32,40},{40,48},{48,56},{56,64},{64,7... | collective-permute-start | bytes 405512 | tf_op jit(solution)/shard_map/ppermute | solution.py:27
  257.3 218.4 %collective-permute-start.17 = (f32[66,512]{1,0:T(8,128)}, f32[66,512]{1,0:T(8,128)S(1)}, u32[]{:S(2)}, u32[]{:S(2)}) collective-permute-start(f32[66,512]{1,0:T(8,128)} %get-tuple-element.70), channel_id=1, source_target_pairs={{8,0},{16,8},{24,16},{32,24},{40,32},{48,40},{56,48},{64,56},{72,6... | collective-permute-start | bytes 405512 | tf_op jit(solution)/shard_map/ppermute | solution.py:29
  312.8 125.2 %collective-permute-start.10 = (f32[388,66]{1,0:T(8,128)S(1)}, f32[388,66]{1,0:T(8,128)S(1)}, u32[]{:S(2)}, u32[]{:S(2)}) collective-permute-start(f32[388,66]{1,0:T(8,128)S(1)} %get-tuple-element.47), channel_id=1, source_target_pairs={{0,1},{1,2},{2,3},{3,4},{4,5},{5,6},{6,7},{7,0},{8,9},{9,10},{10,1... | collective-permute-start | bytes 307304 | tf_op jit(solution)/shard_map/ppermute | solution.py:27
  313.3 124.8 %collective-permute-start.11 = (f32[388,66]{1,0:T(8,128)S(1)}, f32[388,66]{1,0:T(8,128)S(1)}, u32[]{:S(2)}, u32[]{:S(2)}) collective-permute-start(f32[388,66]{1,0:T(8,128)S(1)} %get-tuple-element.48), channel_id=1, source_target_pairs={{1,0},{2,1},{3,2},{4,3},{5,4},{6,5},{7,6},{0,7},{9,8},{10,9},{11,1... | collective-permute-start | bytes 307304 | tf_op jit(solution)/shard_map/ppermute | solution.py:29
  469.8 9.6 %collective-permute-start.12 = (f32[66,512]{1,0:T(8,128)S(1)}, f32[66,512]{1,0:T(8,128)S(1)}, u32[]{:S(2)}, u32[]{:S(2)}) collective-permute-start(f32[66,512]{1,0:T(8,128)S(1)} %get-tuple-element.61), channel_id=1, source_target_pairs={{0,8},{8,16},{16,24},{24,32},{32,40},{40,48},{48,56},{56,64},{64,7... | collective-permute-start | bytes 405512 | tf_op jit(solution)/shard_map/ppermute | solution.py:27
  469.9 9.5 %collective-permute-start.13 = (f32[66,512]{1,0:T(8,128)S(1)}, f32[66,512]{1,0:T(8,128)S(1)}, u32[]{:S(2)}, u32[]{:S(2)}) collective-permute-start(f32[66,512]{1,0:T(8,128)S(1)} %get-tuple-element.62), channel_id=1, source_target_pairs={{8,0},{16,8},{24,16},{32,24},{40,32},{48,40},{56,48},{64,56},{72,6... | collective-permute-start | bytes 405512 | tf_op jit(solution)/shard_map/ppermute | solution.py:29
  634.1 10.1 %collective-permute-start.20 = (f32[66,512]{1,0:T(8,128)S(1)}, f32[66,512]{1,0:T(8,128)S(1)}, u32[]{:S(2)}, u32[]{:S(2)}) collective-permute-start(f32[66,512]{1,0:T(8,128)S(1)} %get-tuple-element.59), channel_id=1, source_target_pairs={{0,8},{8,16},{16,24},{24,32},{32,40},{40,48},{48,56},{56,64},{64,7... | collective-permute-start | bytes 405512 | tf_op jit(solution)/shard_map/ppermute | solution.py:27
  634.2 10.2 %collective-permute-start.21 = (f32[66,512]{1,0:T(8,128)S(1)}, f32[66,512]{1,0:T(8,128)S(1)}, u32[]{:S(2)}, u32[]{:S(2)}) collective-permute-start(f32[66,512]{1,0:T(8,128)S(1)} %get-tuple-element.60), channel_id=1, source_target_pairs={{8,0},{16,8},{24,16},{32,24},{40,32},{48,40},{56,48},{64,56},{72,6... | collective-permute-start | bytes 405512 | tf_op jit(solution)/shard_map/ppermute | solution.py:29
  645.2 14.7 %collective-permute-start.22 = (f32[388,66]{1,0:T(8,128)}, f32[388,66]{1,0:T(8,128)S(1)}, u32[]{:S(2)}, u32[]{:S(2)}) collective-permute-start(f32[388,66]{1,0:T(8,128)} %get-tuple-element.43), channel_id=1, source_target_pairs={{0,1},{1,2},{2,3},{3,4},{4,5},{5,6},{6,7},{7,0},{8,9},{9,10},{10,1... | collective-permute-start | bytes 307304 | tf_op jit(solution)/shard_map/ppermute | solution.py:27
  645.2 14.7 %collective-permute-start.23 = (f32[388,66]{1,0:T(8,128)S(1)}, f32[388,66]{1,0:T(8,128)}, u32[]{:S(2)}, u32[]{:S(2)}) collective-permute-start(f32[388,66]{1,0:T(8,128)S(1)} %get-tuple-element.44), channel_id=1, source_target_pairs={{1,0},{2,1},{3,2},{4,3},{5,4},{6,5},{7,6},{0,7},{9,8},{10,9},{11,1... | collective-permute-start | bytes 307304 | tf_op jit(solution)/shard_map/ppermute | solution.py:29
  687.5 8.3 collective-permute-start.24
  687.6 8.7 %collective-permute-start.25 = (f32[66,512]{1,0:T(8,128)S(1)}, f32[66,512]{1,0:T(8,128)S(1)}, u32[]{:S(2)}, u32[]{:S(2)}) collective-permute-start(f32[66,512]{1,0:T(8,128)S(1)} %get-tuple-element.58), channel_id=1, source_target_pairs={{8,0},{16,8},{24,16},{32,24},{40,32},{48,40},{56,48},{64,56},{72,6... | collective-permute-start | bytes 405512 | tf_op jit(solution)/shard_map/ppermute | solution.py:29
  697.1 14.2 %collective-permute-start.26 = (f32[388,66]{1,0:T(8,128)}, f32[388,66]{1,0:T(8,128)}, u32[]{:S(2)}, u32[]{:S(2)}) collective-permute-start(f32[388,66]{1,0:T(8,128)} %get-tuple-element.41), channel_id=1, source_target_pairs={{0,1},{1,2},{2,3},{3,4},{4,5},{5,6},{6,7},{7,0},{8,9},{9,10},{10,1... | collective-permute-start | bytes 307304 | tf_op jit(solution)/shard_map/ppermute | solution.py:27
  697.1 14.2 %collective-permute-start.27 = (f32[388,66]{1,0:T(8,128)}, f32[388,66]{1,0:T(8,128)}, u32[]{:S(2)}, u32[]{:S(2)}) collective-permute-start(f32[388,66]{1,0:T(8,128)} %get-tuple-element.42), channel_id=1, source_target_pairs={{1,0},{2,1},{3,2},{4,3},{5,4},{6,5},{7,6},{0,7},{9,8},{10,9},{11,1... | collective-permute-start | bytes 307304 | tf_op jit(solution)/shard_map/ppermute | solution.py:29
  738.7 8.8 %collective-permute-start.28 = (f32[66,512]{1,0:T(8,128)S(1)}, f32[66,512]{1,0:T(8,128)S(1)}, u32[]{:S(2)}, u32[]{:S(2)}) collective-permute-start(f32[66,512]{1,0:T(8,128)S(1)} %get-tuple-element.55), channel_id=1, source_target_pairs={{0,8},{8,16},{16,24},{24,32},{32,40},{40,48},{48,56},{56,64},{64,7... | collective-permute-start | bytes 405512 | tf_op jit(solution)/shard_map/ppermute | solution.py:27
  738.7 9.0 %collective-permute-start.29 = (f32[66,512]{1,0:T(8,128)S(1)}, f32[66,512]{1,0:T(8,128)S(1)}, u32[]{:S(2)}, u32[]{:S(2)}) collective-permute-start(f32[66,512]{1,0:T(8,128)S(1)} %get-tuple-element.56), channel_id=1, source_target_pairs={{8,0},{16,8},{24,16},{32,24},{40,32},{48,40},{56,48},{64,56},{72,6... | collective-permute-start | bytes 405512 | tf_op jit(solution)/shard_map/ppermute | solution.py:29
  748.5 14.1 %collective-permute-start.30 = (f32[388,66]{1,0:T(8,128)}, f32[388,66]{1,0:T(8,128)}, u32[]{:S(2)}, u32[]{:S(2)}) collective-permute-start(f32[388,66]{1,0:T(8,128)} %get-tuple-element.39), channel_id=1, source_target_pairs={{0,1},{1,2},{2,3},{3,4},{4,5},{5,6},{6,7},{7,0},{8,9},{9,10},{10,1... | collective-permute-start | bytes 307304 | tf_op jit(solution)/shard_map/ppermute | solution.py:27
  748.5 14.1 %collective-permute-start.31 = (f32[388,66]{1,0:T(8,128)}, f32[388,66]{1,0:T(8,128)}, u32[]{:S(2)}, u32[]{:S(2)}) collective-permute-start(f32[388,66]{1,0:T(8,128)} %get-tuple-element.40), channel_id=1, source_target_pairs={{1,0},{2,1},{3,2},{4,3},{5,4},{6,5},{7,6},{0,7},{9,8},{10,9},{11,1... | collective-permute-start | bytes 307304 | tf_op jit(solution)/shard_map/ppermute | solution.py:29
  (38 other events, 542.6 us)
where the time goes:
time: 847 us; the launch traced here: 831 us
  between operations  362 us (43%)
  other arithmetic  332 us (39%)
  starting transfers between devices  82.6 us (10%)
  blocking collectives  34.5 us (4%)
  waiting for transfers between devices  10.8 us (1%)
  local copies, waits for them, and re-layouts  8.89 us (1%)
    reduce_sum x4, other arithmetic, shards(): local_sums.append(jnp.sum(arrived))  224 us
    min x3, other arithmetic, policy(): lowest = reduce(jnp.minimum, candidates)  93.1 us
    ppermute x16, starting transfers between devices, with_halo(): lax.ppermute(head, axis, [((i + 1) % count, i) for i in range(count)])  69.7 us
    psum x5, blocking collectives, by_axis(): x = lax.psum(x, axis)  34.5 us
  transfers between devices with their start and end apart: 32, of which 9 were waited for; matrix products, arithmetic and copies ran while one was open for 5% of the time, Pallas kernels for 0%

commit v1 on v0

v1 whole, which is shorter than its diff:
```python
import functools

import jax
import jax.numpy as jnp
from jax import lax
from jax.experimental import pallas as pl
from jax.experimental.pallas import tpu as pltpu
from jax.sharding import PartitionSpec as P

MESH = pl.DeviceIdType.MESH
LANES = 128
HALO = 72
CHUNK = 64
GROWS = CHUNK + 8
PIECE = 24

time_step = 0.1
temper = 0.3
epsilon = 1e-06


def catmull(t):
    square = t * t
    last = (0.5 * t) * (square - t)
    first = 0.5 * (square - t) - last
    third = 0.5 * (square + t) - 3.0 * last
    second = 1.0 - first - third - last
    return [first, second, third, last]


def kernel(
    off, cost, term, crowd, dens, frac,
    value_out, mass_out, sums,
    ea, eb, ec, ga, gb, wts, ramps, recip, cr, fr,
    load_sem, send_sem, recv_sem,
):
    rows, cols = term.shape
    tiles = cols // LANES
    steps, controls = cost.shape
    chunks = rows // CHUNK
    nx, ny = lax.axis_size("gx"), lax.axis_size("gy")
    x, y = lax.axis_index("gx"), lax.axis_index("gy")
    up, down = lax.rem(x + nx - 1, nx), lax.rem(x + 1, nx)
    left, right = lax.rem(y + ny - 1, ny), lax.rem(y + 1, ny)
    lane = lax.broadcasted_iota(jnp.int32, (PIECE, LANES), 1)

    barrier = pltpu.get_barrier_semaphore()
    around = [(i, j) for i in (up, x, down) for j in (left, y, right)]
    around.pop(4)
    for i, j in around:
        pl.semaphore_signal(barrier, inc=1, device_id=(i, j), device_id_type=MESH)

    def load_field(src, buf, first):
        return [
            pltpu.make_async_copy(
                src.at[:, pl.ds(c * LANES, LANES)],
                buf.at[1 + c, pl.ds(HALO, rows), :],
                load_sem.at[first + c],
            )
            for c in range(tiles)
        ]

    load_term = load_field(term, ea, 0)
    load_dens = load_field(dens, ec, tiles)
    load_cr = pltpu.make_async_copy(crowd, cr, load_sem.at[2 * tiles])
    load_fr = [
        pltpu.make_async_copy(frac.at[n], fr.at[n], load_sem.at[2 * tiles + 1 + n])
        for n in range(steps)
    ]
    for copy in load_term:
        copy.start()
    load_fr[steps - 1].start()
    load_cr.start()
    for copy in load_fr[: steps - 1]:
        copy.start()
    for copy in load_dens:
        copy.start()

    low, high = HALO, HALO + rows
    mid = pl.ds(1, tiles)

    def exchange(buf, slot):
        def send(index, src_tile, src_row, dst_tile, dst_row, count, i, j):
            return pltpu.make_async_remote_copy(
                src_ref=buf.at[src_tile, pl.ds(src_row, count), :],
                dst_ref=buf.at[dst_tile, pl.ds(dst_row, count), :],
                send_sem=send_sem.at[slot, index],
                recv_sem=recv_sem.at[slot, index],
                device_id=(i, j),
                device_id_type=MESH,
            )

        one, many, end = pl.ds(1, 1), pl.ds(tiles, 1), pl.ds(tiles + 1, 1)
        zero = pl.ds(0, 1)
        north = [
            send(0, mid, low, mid, high, HALO, up, y),
            send(2, one, low, end, high, HALO, up, left),
            send(3, many, low, zero, high, HALO, up, right),
        ]
        south = [
            send(1, mid, high - HALO, mid, 0, HALO, down, y),
            send(4, one, high - HALO, end, 0, HALO, down, left),
            send(5, many, high - HALO, zero, 0, HALO, down, right),
        ]
        sides = []
        for q in range(chunks):
            r = low + q * CHUNK
            sides.append(
                [
                    send(6 + q, one, r, end, r, CHUNK, x, left),
                    send(6 + chunks + q, many, r, zero, r, CHUNK, x, right),
                ]
            )
        return north, south, sides

    def every(buf, slot):
        north, south, sides = exchange(buf, slot)
        return north + south + [d for pair in sides for d in pair]

    def weights_pass(n):
        def body(i, _):
            r = pl.ds(pl.multiple_of(i * 8, 8), 8)
            for c in range(tiles):
                lanes = pl.ds(c * LANES, LANES)
                wx = catmull(fr[n, 0, r, lanes])
                wy = catmull(fr[n, 1, r, lanes])
                for a in range(4):
                    for b in range(4):
                        wts[a * 4 + b, c, r, :] = wx[a] * wy[b]
            return 0

        lax.fori_loop(0, rows // 8, body, 0)

    def shift(src, dst, n, k, row0, sign):
        a, b = sign * off[n, k, 0], sign * off[n, k, 1]
        start = HALO + row0 + a - 1
        for s in range(4):
            total = LANES + b + s - 1
            tile = lax.shift_right_logical(total, 7)
            by = lax.bitwise_and(total, LANES - 1)
            amount = lax.bitwise_and(LANES - by, LANES - 1)
            keep = lane < LANES - by
            for p in range(0, GROWS, PIECE):
                turned = [
                    pltpu.roll(src[tile + c, pl.ds(start + p, PIECE), :], amount, 1)
                    for c in range(tiles + 1)
                ]
                for c in range(tiles):
                    dst[k, s, c, p : p + PIECE, :] = jnp.where(keep, turned[c], turned[c + 1])

    def sample(src, w, k, c, j):
        acc = None
        for a in range(4):
            for b in range(4):
                part = w[a * 4 + b] * src[k, b, c, pl.ds(j + a, 8), :]
                acc = part if acc is None else acc + part
        return acc

    def backward_rows(src, dst, n, row0, i):
        j = pl.multiple_of(i * 8, 8)
        r = pl.ds(pl.multiple_of(row0 + j, 8), 8)
        for c in range(tiles):
            w = [wts[m, c, r, :] for m in range(16)]
            q = [sample(src, w, k, c, j) + time_step * cost[n, k] for k in range(controls)]
            lowest = functools.reduce(jnp.minimum, q)
            edge = lowest + temper
            total = None
            for k in range(controls):
                ramp = jnp.maximum(edge - q[k], 0.0)
                ramps[n * controls + k, c, r, :] = ramp
                total = ramp if total is None else total + ramp
            recip[n, c, r, :] = 1.0 / total
            here = pl.ds(pl.multiple_of(HALO + row0 + j, 8), 8)
            dst[1 + c, here, :] = lowest + time_step * cr[r, pl.ds(c * LANES, LANES)]

    def forward_rows(src, dst, n, row0, i):
        j = pl.multiple_of(i * 8, 8)
        r = pl.ds(pl.multiple_of(row0 + j, 8), 8)
        added = sums[n]
        for c in range(tiles):
            w = [wts[m, c, r, :] for m in range(16)]
            acc = None
            for k in range(controls):
                part = ramps[n * controls + k, c, r, :] * sample(src, w, k, c, j)
                acc = part if acc is None else acc + part
            acc = jnp.maximum(acc * recip[n, c, r, :], 0.0)
            here = pl.ds(pl.multiple_of(HALO + row0 + j, 8), 8)
            dst[1 + c, here, :] = acc
            added = added + acc
        sums[n] = added

    order = [0, chunks - 1] + list(range(1, chunks - 1))

    def stage(src, dst, slot_src, slot_dst, n, sign, rows_fn, send):
        weights_pass(n)
        for d in every(src, slot_src):
            d.wait()
        north, south, sides = exchange(dst, slot_dst)

        def first(k, _):
            shift(src, ga, n, k, order[0] * CHUNK, sign)
            return 0

        lax.fori_loop(0, controls, first, 0)
        now, later = ga, gb
        for at, q in enumerate(order):
            following = order[at + 1] if at + 1 < chunks else None

            def body(i, _):
                rows_fn(now, dst, n, q * CHUNK, i)
                if following is not None:
                    shift(src, later, n, i, following * CHUNK, sign)
                return 0

            lax.fori_loop(0, CHUNK // 8, body, 0)
            now, later = later, now
            todo = list(sides[q])
            if q == 1:
                todo += north
            if q == chunks - 2:
                todo += south

            def go():
                for d in todo:
                    d.start()

            if send is True:
                go()
            else:
                pl.when(send)(go)

    for copy in load_term:
        copy.wait()
    pl.semaphore_wait(barrier, 8)
    for d in every(ea, 0):
        d.start()
    for copy in load_dens:
        copy.wait()
    for d in every(ec, 2):
        d.start()
    load_fr[steps - 1].wait()
    load_cr.wait()
    for copy in load_fr[: steps - 1]:
        copy.wait()
    sums[...] = jnp.zeros_like(sums)

    def backward_pair(m, _):
        n = steps - 1 - 2 * m
        stage(ea, eb, 0, 1, n, 1, backward_rows, True)
        stage(eb, ea, 1, 0, n - 1, 1, backward_rows, m + 1 < steps // 2)
        return 0

    lax.fori_loop(0, steps // 2, backward_pair, 0)

    def store_field(buf, dst, first):
        return [
            pltpu.make_async_copy(
                buf.at[1 + c, pl.ds(HALO, rows), :],
                dst.at[:, pl.ds(c * LANES, LANES)],
                load_sem.at[first + c],
            )
            for c in range(tiles)
        ]

    for copy in store_field(ea, value_out, 0):
        copy.start()
    for copy in store_field(ea, value_out, 0):
        copy.wait()

    def forward_pair(m, _):
        n = 2 * m
        stage(ec, ea, 2, 0, n, -1, forward_rows, True)
        stage(ea, ec, 0, 2, n + 1, -1, forward_rows, m + 1 < steps // 2)
        return 0

    lax.fori_loop(0, steps // 2, forward_pair, 0)
    for copy in store_field(ec, mass_out, tiles):
        copy.start()
    for copy in store_field(ec, mass_out, tiles):
        copy.wait()


def shards(terminal, crowding, density, fractions, offsets, control_cost):
    rows, cols = terminal.shape
    tiles = cols // LANES
    steps, controls = control_cost.shape
    chunks = rows // CHUNK
    cells = rows * cols * lax.axis_size("gx") * lax.axis_size("gy")
    field = jax.ShapeDtypeStruct((rows, cols), jnp.float32)
    copies = 6 + 2 * chunks
    extended = pltpu.VMEM((tiles + 2, rows + 2 * HALO, LANES), jnp.float32)
    shifted = pltpu.VMEM((controls, 4, tiles, GROWS, LANES), jnp.float32)
    smem = pl.BlockSpec(memory_space=pltpu.SMEM)
    hbm = pl.BlockSpec(memory_space=pl.ANY)
    value, mass, sums = pl.pallas_call(
        kernel,
        out_shape=(field, field, jax.ShapeDtypeStruct((steps, 8, LANES), jnp.float32)),
        in_specs=[smem, smem, hbm, hbm, hbm, hbm],
        out_specs=(hbm, hbm, pl.BlockSpec(memory_space=pltpu.VMEM)),
        scratch_shapes=[
            extended, extended, extended, shifted, shifted,
            pltpu.VMEM((16, tiles, rows, LANES), jnp.float32),
            pltpu.VMEM((steps * controls, tiles, rows, LANES), jnp.float32),
            pltpu.VMEM((steps, tiles, rows, LANES), jnp.float32),
            pltpu.VMEM((rows, cols), jnp.float32),
            pltpu.VMEM((steps, 2, rows, cols), jnp.float32),
            pltpu.SemaphoreType.DMA((2 * tiles + 1 + steps,)),
            pltpu.SemaphoreType.DMA((3, copies)),
            pltpu.SemaphoreType.DMA((3, copies)),
        ],
        compiler_params=pltpu.CompilerParams(
            collective_id=0, has_side_effects=True, vmem_limit_bytes=60 * 2**20
        ),
    )(offsets, control_cost, terminal, crowding, density, fractions)
    totals = lax.psum(jnp.sum(sums, axis=(1, 2)), ("gx", "gy")) / cells
    masses, scale = [], jnp.float32(1.0)
    for n in range(steps):
        mean = totals[n] / scale
        masses.append(mean)
        scale = scale * (mean + epsilon)
    return value, mass / scale, jnp.stack(masses)


def solution(mesh):
    placed = (P("gx", "gy"), P("gx", "gy"), P("gx", "gy"), P(None, None, "gx", "gy"), P(), P())
    return jax.shard_map(
        shards,
        mesh=mesh,
        in_specs=placed,
        out_specs=(P("gx", "gy"), P("gx", "gy"), P()),
        check_vma=False,
    )
```

time: 847 us -> 266 us (0.31); the launches traced: 831 us -> 266 us
  between operations: 362 us -> 3.31 us
  other arithmetic: 332 us -> 4.01 us
  Pallas kernels: 0 us -> 190 us
  starting transfers between devices: 82.6 us -> 0 us
  blocking collectives: 34.5 us -> 64.5 us
  waiting for transfers between devices: 10.8 us -> 0 us
    reduce_sum x4 -> x1, other arithmetic: 224 us -> 0.83 us  [shards(): totals = lax.psum(jnp.sum(sums, axis=(1, 2)), ('gx', 'gy')) / cells]
    pallas_call x0 -> x1, Pallas kernels: none -> 190 us  [shards(): pl.pallas_call(kernel, out_shape=(field, field, jax.ShapeDtypeStruct((ste...]
    min x3 -> x0, other arithmetic: 93.1 us -> none  [policy(): lowest = reduce(jnp.minimum, candidates)]
    ppermute x32 -> x0, starting transfers between devices: 82.6 us -> none  [the longest x16 69.7 us: with_halo(): lax.ppermute(head, axis, [((i + 1) % count, i) for i in range(count)])]
    psum x5 -> x1, blocking collectives: 34.5 us -> 64.5 us  [shards(): totals = lax.psum(jnp.sum(sums, axis=(1, 2)), ('gx', 'gy')) / cells]
    ppermute x32 -> x0, waiting for transfers between devices: 10.8 us -> none  [the longest x16 9.85 us: with_halo(): lax.ppermute(tail, axis, [(i, (i + 1) % count) for i in range(count)])]
    concatenate x9 -> x0, other arithmetic: 9.14 us -> none  [the longest x8 7.91 us: with_halo(): jnp.concatenate([lax.ppermute(tail, axis, [(i, (i + 1) % count) for i in...]
  transfers between devices with their start and end apart: 32 -> 0, of which waited for: 9 -> 0; matrix products, arithmetic and copies ran while one was open for 5% -> 0% of each run, Pallas kernels for 0% -> 0%
where the time goes in v1:
time: 266 us
  Pallas kernels  190 us (71%)
  blocking collectives  64.5 us (24%)
  other arithmetic  4.01 us (2%)
  local copies, waits for them, and re-layouts  3.85 us (1%)
  between operations  3.31 us (1%)
    pallas_call x1, Pallas kernels, shards(): pl.pallas_call(kernel, out_shape=(field, field, jax.ShapeDtypeStruct((ste...  190 us
    psum x1, blocking collectives, shards(): totals = lax.psum(jnp.sum(sums, axis=(1, 2)), ('gx', 'gy')) / cells  64.5 us

profile of v1, /device:TPU:1, one launch (start us, length us, event | category | flops | bytes accessed | tf_op | source)
XLA Modules:
  0.0 266.0 jit_solution(7732580850385866216)
XLA Ops:
  0.6 1.4 copy.9.off
  2.0 190.3 %shard_map.85 = (f32[256,512]{1,0:T(8,128)}, f32[256,512]{1,0:T(8,128)}, f32[4,8,128]{2,1,0:T(8,128)}) custom-call(s32[4,8,2]{2,1,0:T(8,128)} %copy.9.off, f32[4,8]{1,0:T(4,128)} %cost.1, f32[256,512]{1,0:T(8,128)} %term.1, f32[256,512]{1,0:T(8,128)} %crowd.1, f32[256,512]{1,0:T(8,128)} %dens.1, f32[4,2,256,512]{3,2,1,0:T(8,128)} %frac.1), custom_call_target="tpu_custom_call" | custom-call | tf_op jit(solution)/shard_map/pallas_call | solution.py:295
  192.3 0.8 reduce_sum.9
  193.1 64.5 %psum.7 = f32[4]{0:T(128)S(1)} all-reduce(f32[4]{0:T(128)S(1)} %reduce_sum.9), channel_id=1, replica_groups=mesh['gx'=16,'gy'=8] {'gx','gy'}, use_global_device_ids=true, to_apply=%region_1.0 | all-reduce | flops 4 | bytes 32 | tf_op jit(solution)/shard_map/psum | solution.py:315
  257.7 0.6 fusion
  260.9 1.3 pad_maximum_fusion
  262.2 1.9 broadcast_divide_fusion
  264.1 1.9 copy.11
  (1 shorter events, 0.0 us)

commit v2 on v1

v2 whole, which is shorter than its diff:
```python
import functools

import jax
import jax.numpy as jnp
from jax import lax
from jax.experimental import pallas as pl
from jax.experimental.pallas import tpu as pltpu
from jax.sharding import PartitionSpec as P

MESH = pl.DeviceIdType.MESH
LANES = 128
HALO = 72
PIECE = 24
BLOCK = 64
EDGE = 32

time_step = 0.1
temper = 0.3
epsilon = 1e-06


def catmull(t):
    square = t * t
    last = (0.5 * t) * (square - t)
    first = 0.5 * (square - t) - last
    third = 0.5 * (square + t) - 3.0 * last
    second = 1.0 - first - third - last
    return [first, second, third, last]


def kernel(
    off, cost, term, crowd, dens, frac,
    value_out, mass_out, masses_out,
    sums, part_y, part_x, ea, eb, ec, strips, packs, halo, moved,
    wts, ramps, recip, cr, fr, stage_a, stage_b, order,
    load_sem, send_sem, recv_sem, sum_send, sum_recv,
):
    rows, cols = term.shape
    tiles = cols // LANES
    taps = tiles + 3
    groups = rows // 8
    steps, controls = cost.shape
    nx, ny = lax.axis_size("gx"), lax.axis_size("gy")
    x, y = lax.axis_index("gx"), lax.axis_index("gy")
    up, down = lax.rem(x + nx - 1, nx), lax.rem(x + 1, nx)
    left, right = lax.rem(y + ny - 1, ny), lax.rem(y + 1, ny)
    low, high = HALO, HALO + rows

    def lanes_of(count):
        return lax.broadcasted_iota(jnp.int32, (count, LANES), 1)

    load_term = pltpu.make_async_copy(term, stage_a, load_sem.at[0])
    load_dens = pltpu.make_async_copy(dens, stage_b, load_sem.at[1])
    load_cr = pltpu.make_async_copy(crowd, cr, load_sem.at[2])
    load_fr = [
        pltpu.make_async_copy(frac.at[n], fr.at[n], load_sem.at[3 + n]) for n in range(steps)
    ]
    load_term.start()
    load_fr[steps - 1].start()
    load_cr.start()
    load_dens.start()
    for copy in load_fr[: steps - 1]:
        copy.start()

    barrier = pltpu.get_barrier_semaphore()
    around = [(i, j) for i in (up, x, down) for j in (left, y, right)]
    around.pop(4)
    for i, j in around:
        pl.semaphore_signal(barrier, inc=1, device_id=(i, j), device_id_type=MESH)

    def order_rows(i, _):
        here = pl.multiple_of(i * BLOCK, BLOCK)
        source = lax.broadcasted_iota(jnp.int32, (BLOCK, cols), 0) + here
        place = lax.broadcasted_iota(jnp.int32, (BLOCK, cols), 1)
        wanted = tiles * lax.bitwise_and(place, LANES - 1) + lax.shift_right_logical(place, 7)
        order[pl.ds(here, BLOCK), :] = jnp.where(source == wanted, 1.0, 0.0).astype(jnp.bfloat16)
        return 0

    lax.fori_loop(0, cols // BLOCK, order_rows, 0)

    def reorder(value, back):
        out = None
        rest = value
        for part in range(3):
            piece = rest.astype(jnp.bfloat16)
            if part < 2:
                rest = rest - piece.astype(jnp.float32)
            got = lax.dot_general(
                piece, order[...], (((1,), (1 if back else 0,)), ((), ())),
                preferred_element_type=jnp.float32,
            )
            out = got if out is None else out + got
        return out

    def each_block(body):
        def step(i, _):
            body(pl.multiple_of(i * BLOCK, BLOCK))
            return 0

        lax.fori_loop(0, rows // BLOCK, step, 0)

    def enter(src, buf):
        def body(r):
            got = reorder(src[pl.ds(r, BLOCK), :], False)
            here = pl.ds(pl.multiple_of(HALO + r, 8), BLOCK)
            for c in range(tiles):
                buf[c, here, :] = got[:, c * LANES : (c + 1) * LANES]

        each_block(body)

    def leave(buf, dst, factor):
        def body(r):
            here = pl.ds(pl.multiple_of(HALO + r, 8), BLOCK)
            whole = jnp.concatenate([buf[c, here, :] for c in range(tiles)], axis=1)
            if factor is not None:
                whole = whole * factor
            dst[pl.ds(r, BLOCK), :] = reorder(whole, True)

        each_block(body)

    def in_place(ref):
        def body(r):
            ref[pl.ds(r, BLOCK), :] = reorder(ref[pl.ds(r, BLOCK), :], False)

        each_block(body)

    def pack(buf, slot, first, count):
        lane = lanes_of(8 * count)
        here = slice(HALO + 8 * first, HALO + 8 * (first + count))
        there = slice(8 * first, 8 * (first + count))
        tile = [buf[c, here, :] for c in range(tiles)]
        for side in range(2):
            out = None
            for c in range(tiles):
                by = EDGE * (c + side) % LANES
                turned = pltpu.roll(tile[c], by, 1) if by else tile[c]
                out = turned if out is None else jnp.where(lane < EDGE * c, out, turned)
            packs[slot, side, there, :] = out

    def unpack(slot):
        def body(i, _):
            r = pl.ds(pl.multiple_of(i * 40, 8), 40)
            lane = lanes_of(40)
            near, far = strips[slot, 0, r, :], strips[slot, 1, r, :]
            for c in range(tiles):
                by, bx = (LANES - EDGE * c) % LANES, EDGE * (tiles - 1 - c)
                a = pltpu.roll(near, by, 1) if by else near
                b = pltpu.roll(far, bx, 1) if bx else far
                halo[c, r, :] = jnp.where(lane < LANES // 2, a, b)
            return 0

        lax.fori_loop(0, (rows + 2 * HALO) // 40, body, 0)

    def exchange(buf, slot):
        def send(index, src, dst, i, j):
            return pltpu.make_async_remote_copy(
                src_ref=src,
                dst_ref=dst,
                send_sem=send_sem.at[slot, index],
                recv_sem=recv_sem.at[slot, index],
                device_id=(i, j),
                device_id_type=MESH,
            )

        def side(index, which, src_row, dst_row, count, i, j):
            return send(
                index,
                packs.at[slot, which, pl.ds(src_row, count), :],
                strips.at[slot, which, pl.ds(dst_row, count), :],
                i, j,
            )

        last = rows - HALO
        outer = [
            send(0, buf.at[:, pl.ds(low, HALO), :], buf.at[:, pl.ds(high, HALO), :], up, y),
            send(1, buf.at[:, pl.ds(high - HALO, HALO), :], buf.at[:, pl.ds(0, HALO), :], down, y),
            side(2, 0, 0, low, HALO, x, left),
            side(3, 1, 0, low, HALO, x, right),
            side(4, 0, last, low + last, HALO, x, left),
            side(5, 1, last, low + last, HALO, x, right),
            side(6, 0, 0, high, HALO, up, left),
            side(7, 1, 0, high, HALO, up, right),
            side(8, 0, last, 0, HALO, down, left),
            side(9, 1, last, 0, HALO, down, right),
        ]
        inner = [
            side(10, 0, HALO, low + HALO, rows - 2 * HALO, x, left),
            side(11, 1, HALO, low + HALO, rows - 2 * HALO, x, right),
        ]
        return outer, inner

    rim, core = HALO // 8, (rows - 2 * HALO) // 8

    def pack_outer(buf, slot):
        pack(buf, slot, 0, rim)
        pack(buf, slot, groups - rim, rim)

    def pack_inner(buf, slot):
        half = core // 2
        pack(buf, slot, rim, half)
        pack(buf, slot, rim + half, core - half)

    def weights_pass(n):
        def body(i, _):
            r = pl.ds(pl.multiple_of(i * 8, 8), 8)
            for c in range(tiles):
                lanes = pl.ds(c * LANES, LANES)
                wx = catmull(fr[n, 0, r, lanes])
                wy = catmull(fr[n, 1, r, lanes])
                for a in range(4):
                    for b in range(4):
                        wts[c, i, a * 4 + b] = wx[a] * wy[b]
            return 0

        lax.fori_loop(0, groups, body, 0)

    def shift(src, n, k, sign):
        a, b = sign * off[n, k, 0], sign * off[n, k, 1]
        start = HALO + a - 1
        lane = lanes_of(PIECE)
        for m in range(taps):
            total = b + (m - 1)
            tile = lax.bitwise_and(total, tiles - 1)
            by = lax.shift_right_arithmetic(total, tiles.bit_length() - 1)
            amount = lax.bitwise_and(-by, LANES - 1)
            inside = lane - by
            mine = jnp.logical_and(inside >= 0, inside < LANES)
            for p in range(0, rows + 8, PIECE):
                r = pl.ds(start + p, PIECE)
                both = jnp.where(mine, src[tile, r, :], halo[tile, r, :])
                moved[k, m, p : p + PIECE, :] = pltpu.roll(both, amount, 1)

    def sample(w, k, c, j):
        acc = None
        for a in range(4):
            for b in range(4):
                part = w[a * 4 + b] * moved[k, c + b, pl.ds(j + a, 8), :]
                acc = part if acc is None else acc + part
        return acc

    def backward_rows(dst, n, g):
        j = pl.multiple_of(g * 8, 8)
        here = pl.ds(pl.multiple_of(HALO + j, 8), 8)
        for c in range(tiles):
            w = [wts[c, g, m] for m in range(16)]
            q = [sample(w, k, c, j) + time_step * cost[n, k] for k in range(controls)]
            lowest = functools.reduce(jnp.minimum, q)
            edge = lowest + temper
            total = None
            for k in range(controls):
                ramp = jnp.maximum(edge - q[k], 0.0)
                ramps[n, c, g, k] = ramp
                total = ramp if total is None else total + ramp
            recip[n, c, g] = 1.0 / total
            dst[c, here, :] = lowest + time_step * cr[pl.ds(j, 8), pl.ds(c * LANES, LANES)]

    def forward_rows(dst, n, g):
        j = pl.multiple_of(g * 8, 8)
        here = pl.ds(pl.multiple_of(HALO + j, 8), 8)
        added = sums[n]
        for c in range(tiles):
            w = [wts[c, g, m] for m in range(16)]
            acc = None
            for k in range(controls):
                part = ramps[n, c, g, k] * sample(w, k, c, j)
                acc = part if acc is None else acc + part
            acc = jnp.maximum(acc * recip[n, c, g], 0.0)
            dst[c, here, :] = acc
            added = added + acc
        sums[n] = added

    def wait_all(buf, slot):
        outer, inner = exchange(buf, slot)
        for d in outer + inner:
            d.wait()

    def stage(src, dst, slot_src, slot_dst, n, sign, rows_fn, send, fresh):
        if fresh:
            in_place(fr.at[n, 0])
            in_place(fr.at[n, 1])
        weights_pass(n)
        wait_all(src, slot_src)
        unpack(slot_src)

        def shifts(k, _):
            shift(src, n, k, sign)
            return 0

        lax.fori_loop(0, controls, shifts, 0)
        outer, inner = exchange(dst, slot_dst)

        def publish(pack_fn, copies):
            def go():
                pack_fn(dst, slot_dst)
                for d in copies:
                    d.start()

            if send is True:
                go()
            else:
                pl.when(send)(go)

        def outer_rows(t, _):
            rows_fn(dst, n, t + core * (t // rim))
            return 0

        def inner_rows(t, _):
            rows_fn(dst, n, t + rim)
            return 0

        lax.fori_loop(0, 2 * rim, outer_rows, 0)
        publish(pack_outer, outer)
        lax.fori_loop(0, core, inner_rows, 0)
        publish(pack_inner, inner)

    def begin(load, src, buf, slot):
        load.wait()
        enter(src, buf)
        pack_outer(buf, slot)
        pack_inner(buf, slot)
        return [d for part in exchange(buf, slot) for d in part]

    first = begin(load_term, stage_a, ea, 0)
    pl.semaphore_wait(barrier, 8)
    for d in first:
        d.start()
    for d in begin(load_dens, stage_b, ec, 2):
        d.start()
    load_cr.wait()
    in_place(cr)
    for copy in load_fr:
        copy.wait()
    sums[...] = jnp.zeros_like(sums)

    def backward_pair(m, _):
        n = steps - 1 - 2 * m
        stage(ea, eb, 0, 1, n, 1, backward_rows, True, True)
        stage(eb, ea, 1, 0, n - 1, 1, backward_rows, m + 1 < steps // 2, True)
        return 0

    lax.fori_loop(0, steps // 2, backward_pair, 0)
    leave(ea, stage_a, None)
    store_value = pltpu.make_async_copy(stage_a, value_out, load_sem.at[0])
    store_value.start()

    def forward_pair(m, _):
        n = 2 * m
        stage(ec, ea, 2, 0, n, -1, forward_rows, True, False)
        stage(ea, ec, 0, 2, n + 1, -1, forward_rows, m + 1 < steps // 2, False)
        return 0

    lax.fori_loop(0, steps // 2, forward_pair, 0)

    def spread(part, count, at, own, first):
        copies = []
        for hop in range(1, count):
            copies.append(
                pltpu.make_async_remote_copy(
                    src_ref=part.at[0],
                    dst_ref=part.at[hop],
                    send_sem=sum_send.at[first + hop],
                    recv_sem=sum_recv.at[first + hop],
                    device_id=at(lax.rem(own + hop, count)),
                    device_id_type=MESH,
                )
            )
        for copy in copies:
            copy.start()
        for copy in copies:
            copy.wait()
        total = part[0]
        for hop in range(1, count):
            total = total + part[hop]
        return total

    own = [jnp.sum(sums[n], axis=0, keepdims=True) for n in range(steps)]
    part_y[0] = jnp.concatenate(own + [jnp.zeros((8 - steps, LANES), jnp.float32)], axis=0)
    part_x[0] = spread(part_y, ny, lambda j: (x, j), y, 0)
    whole = spread(part_x, nx, lambda i: (i, y), x, ny)
    totals = jnp.sum(whole, axis=1, keepdims=True) * (1.0 / (rows * cols * nx * ny))
    scale = jnp.ones((1, 1), jnp.float32)
    found = []
    for n in range(steps):
        mean = totals[n : n + 1, :] / scale
        found.append(mean)
        scale = scale * (mean + epsilon)
    found.append(jnp.zeros((8 - steps, 1), jnp.float32))
    masses_out[...] = jnp.broadcast_to(jnp.concatenate(found, axis=0), (8, LANES))
    factor = jnp.broadcast_to(1.0 / scale, (BLOCK, cols))

    leave(ec, stage_b, factor)
    store_mass = pltpu.make_async_copy(stage_b, mass_out, load_sem.at[1])
    store_mass.start()
    store_mass.wait()
    store_value.wait()


def shards(terminal, crowding, density, fractions, offsets, control_cost):
    rows, cols = terminal.shape
    tiles = cols // LANES
    steps, controls = control_cost.shape
    nx, ny = lax.axis_size("gx"), lax.axis_size("gy")
    field = jax.ShapeDtypeStruct((rows, cols), jnp.float32)
    tall = rows + 2 * HALO
    copies = 12

    def vmem(*shape):
        return pltpu.VMEM(shape, jnp.float32)

    smem = pl.BlockSpec(memory_space=pltpu.SMEM)
    hbm = pl.BlockSpec(memory_space=pl.ANY)
    value, mass, masses = pl.pallas_call(
        kernel,
        out_shape=(field, field, jax.ShapeDtypeStruct((8, LANES), jnp.float32)),
        in_specs=[smem, smem, hbm, hbm, hbm, hbm],
        out_specs=(hbm, hbm, pl.BlockSpec(memory_space=pltpu.VMEM)),
        scratch_shapes=[
            vmem(steps, 8, LANES),
            vmem(ny, 8, LANES),
            vmem(nx, 8, LANES),
            vmem(tiles, tall, LANES),
            vmem(tiles, tall, LANES),
            vmem(tiles, tall, LANES),
            vmem(3, 2, tall, LANES),
            vmem(3, 2, rows, LANES),
            vmem(tiles, tall, LANES),
            vmem(controls, tiles + 3, rows + 8, LANES),
            vmem(tiles, rows // 8, 16, 8, LANES),
            vmem(steps, tiles, rows // 8, controls, 8, LANES),
            vmem(steps, tiles, rows // 8, 8, LANES),
            vmem(rows, cols),
            vmem(steps, 2, rows, cols),
            vmem(rows, cols),
            vmem(rows, cols),
            pltpu.VMEM((cols, cols), jnp.bfloat16),
            pltpu.SemaphoreType.DMA((3 + steps,)),
            pltpu.SemaphoreType.DMA((3, copies)),
            pltpu.SemaphoreType.DMA((3, copies)),
            pltpu.SemaphoreType.DMA((nx + ny,)),
            pltpu.SemaphoreType.DMA((nx + ny,)),
        ],
        compiler_params=pltpu.CompilerParams(
            collective_id=0, has_side_effects=True, vmem_limit_bytes=60 * 2**20
        ),
    )(offsets, control_cost, terminal, crowding, density, fractions)
    return value, mass, masses[:steps, 0]


def solution(mesh):
    placed = (P("gx", "gy"), P("gx", "gy"), P("gx", "gy"), P(None, None, "gx", "gy"), P(), P())
    return jax.shard_map(
        shards,
        mesh=mesh,
        in_specs=placed,
        out_specs=(P("gx", "gy"), P("gx", "gy"), P()),
        check_vma=False,
    )
```

time: 266 us -> 157 us (0.59)
  blocking collectives: 64.5 us -> 0 us
  Pallas kernels: 190 us -> 149 us
  other arithmetic: 4.01 us -> 0 us
  between operations: 3.31 us -> 0.64 us
    psum x1 -> x0, blocking collectives: 64.5 us -> none  [shards(): totals = lax.psum(jnp.sum(sums, axis=(1, 2)), ('gx', 'gy')) / cells]
    pallas_call x1, Pallas kernels: 190 us -> 149 us  [shards(): pl.pallas_call(kernel, out_shape=(field, field, jax.ShapeDtypeStruct((8,...]
where the time goes in v2:
time: 157 us; the launch traced here: 156 us
  Pallas kernels  149 us (95%)
  local copies, waits for them, and re-layouts  6.42 us (4%)
    pallas_call x1, Pallas kernels, shards(): pl.pallas_call(kernel, out_shape=(field, field, jax.ShapeDtypeStruct((8,...  149 us
    unnamed x3, local copies, waits for them, and re-layouts  5.12 us

profile of v2, /device:TPU:1, one launch (start us, length us, event | category | flops | bytes accessed | tf_op | source)
XLA Modules:
  0.0 156.2 jit_solution(15570062075857804064)
XLA Ops:
  0.6 1.4 copy.10.off
  2.0 149.2 %shard_map.85 = (f32[256,512]{1,0:T(8,128)}, f32[256,512]{1,0:T(8,128)}, f32[8,128]{1,0:T(8,128)}) custom-call(s32[4,8,2]{2,1,0:T(8,128)} %copy.10.off, f32[4,8]{1,0:T(4,128)} %cost.1, f32[256,512]{1,0:T(8,128)} %term.1, f32[256,512]{1,0:T(8,128)} %crowd.1, f32[256,512]{1,0:T(8,128)} %dens.1, f32[4,2,256,512]{3,2,1,0:T(8,128)} %frac.1), custom_call_target="tpu_custom_call" | custom-call | tf_op jit(solution)/shard_map/pallas_call | solution.py:412
  151.2 1.3 slice_reduce_fusion
  152.5 1.9 %copy.13 = f32[256,512]{1,0:T(8,128)} copy(f32[256,512]{1,0:T(8,128)} %get-tuple-element.12) | data formatting | bytes 1048576
  154.4 1.9 %copy.14 = f32[256,512]{1,0:T(8,128)} copy(f32[256,512]{1,0:T(8,128)} %get-tuple-element.13) | data formatting | bytes 1048576

commit v3 on v2

--- a/solution.py
+++ b/solution.py
@@ -11,8 +11,12 @@
 LANES = 128
 HALO = 72
 PIECE = 24
-BLOCK = 64
+BLOCK = 128
+CHUNK = 64
+GROWS = CHUNK + 8
 EDGE = 32
+LAG = 6
+COPIES = 22
 
 time_step = 0.1
 temper = 0.3
@@ -31,7 +35,7 @@
 def kernel(
     off, cost, term, crowd, dens, frac,
     value_out, mass_out, masses_out,
-    sums, part_y, part_x, ea, eb, ec, strips, packs, halo, moved,
+    sums, part_y, part_x, ea, eb, ec, ends, strips, packs, ga, gb,
     wts, ramps, recip, cr, fr, stage_a, stage_b, order,
     load_sem, send_sem, recv_sem, sum_send, sum_recv,
 ):
@@ -79,18 +83,18 @@
     lax.fori_loop(0, cols // BLOCK, order_rows, 0)
 
     def reorder(value, back):
-        out = None
+        count = value.shape[0]
+        pieces = []
         rest = value
         for part in range(3):
-            piece = rest.astype(jnp.bfloat16)
+            pieces.append(rest.astype(jnp.bfloat16))
             if part < 2:
-                rest = rest - piece.astype(jnp.float32)
-            got = lax.dot_general(
-                piece, order[...], (((1,), (1 if back else 0,)), ((), ())),
-                preferred_element_type=jnp.float32,
-            )
-            out = got if out is None else out + got
-        return out
+                rest = rest - pieces[-1].astype(jnp.float32)
+        got = lax.dot_general(
+            jnp.concatenate(pieces, axis=0), order[...], (((1,), (1 if back else 0,)), ((), ())),
+            preferred_element_type=jnp.float32,
+        )
+        return got[:count] + got[count : 2 * count] + got[2 * count :]
 
     def each_block(body):
         def step(i, _):
@@ -137,68 +141,89 @@
                 out = turned if out is None else jnp.where(lane < EDGE * c, out, turned)
             packs[slot, side, there, :] = out
 
-    def unpack(slot):
+    def unpack(buf, slot, first, last, turns):
+        unit = 8 * (last - first) // turns
+
         def body(i, _):
-            r = pl.ds(pl.multiple_of(i * 40, 8), 40)
-            lane = lanes_of(40)
+            r = pl.ds(pl.multiple_of(first * 8 + i * unit, 8), unit)
+            lane = lanes_of(unit)
             near, far = strips[slot, 0, r, :], strips[slot, 1, r, :]
             for c in range(tiles):
                 by, bx = (LANES - EDGE * c) % LANES, EDGE * (tiles - 1 - c)
                 a = pltpu.roll(near, by, 1) if by else near
                 b = pltpu.roll(far, bx, 1) if bx else far
-                halo[c, r, :] = jnp.where(lane < LANES // 2, a, b)
+                buf[tiles + c, r, :] = jnp.where(lane < LANES // 2, a, b)
             return 0
 
-        lax.fori_loop(0, (rows + 2 * HALO) // 40, body, 0)
+        lax.fori_loop(0, turns, body, 0)
+
+    def take_end(buf, slot, side):
+        start = (0, high)[side]
+        for c in range(tiles):
+            buf[c, start : start + HALO, :] = ends[slot, side, c]
 
     def exchange(buf, slot):
-        def send(index, src, dst, i, j):
+        index = iter(range(COPIES))
+
+        def send(src, dst, i, j):
+            at = next(index)
             return pltpu.make_async_remote_copy(
                 src_ref=src,
                 dst_ref=dst,
-                send_sem=send_sem.at[slot, index],
-                recv_sem=recv_sem.at[slot, index],
+                send_sem=send_sem.at[slot, at],
+                recv_sem=recv_sem.at[slot, at],
                 device_id=(i, j),
                 device_id_type=MESH,
             )
 
-        def side(index, which, src_row, dst_row, count, i, j):
-            return send(
-                index,
-                packs.at[slot, which, pl.ds(src_row, count), :],
-                strips.at[slot, which, pl.ds(dst_row, count), :],
-                i, j,
-            )
-
-        last = rows - HALO
-        outer = [
-            send(0, buf.at[:, pl.ds(low, HALO), :], buf.at[:, pl.ds(high, HALO), :], up, y),
-            send(1, buf.at[:, pl.ds(high - HALO, HALO), :], buf.at[:, pl.ds(0, HALO), :], down, y),
-            side(2, 0, 0, low, HALO, x, left),
-            side(3, 1, 0, low, HALO, x, right),
-            side(4, 0, last, low + last, HALO, x, left),
-            side(5, 1, last, low + last, HALO, x, right),
-            side(6, 0, 0, high, HALO, up, left),
-            side(7, 1, 0, high, HALO, up, right),
-            side(8, 0, last, 0, HALO, down, left),
-            side(9, 1, last, 0, HALO, down, right),
-        ]
-        inner = [
-            side(10, 0, HALO, low + HALO, rows - 2 * HALO, x, left),
-            side(11, 1, HALO, low + HALO, rows - 2 * HALO, x, right),
-        ]
-        return outer, inner
-
-    rim, core = HALO // 8, (rows - 2 * HALO) // 8
-
-    def pack_outer(buf, slot):
-        pack(buf, slot, 0, rim)
-        pack(buf, slot, groups - rim, rim)
-
-    def pack_inner(buf, slot):
-        half = core // 2
-        pack(buf, slot, rim, half)
-        pack(buf, slot, rim + half, core - half)
+        def rows_to(first, count, start, i):
+            return [
+                send(
+                    packs.at[slot, which, pl.ds(first, count), :],
+                    strips.at[slot, which, pl.ds(start, count), :],
+                    i, j,
+                )
+                for which, j in ((0, left), (1, right))
+            ]
+
+        def north(first, count):
+            return [
+                send(
+                    buf.at[pl.ds(0, tiles), pl.ds(low + first, count), :],
+                    ends.at[slot, 1, :, pl.ds(first, count), :],
+                    up, y,
+                )
+            ] + rows_to(first, count, high + first, up)
+
+        def south(first, count):
+            start = first - (rows - HALO)
+            return [
+                send(
+                    buf.at[pl.ds(0, tiles), pl.ds(low + first, count), :],
+                    ends.at[slot, 0, :, pl.ds(start, count), :],
+                    down, y,
+                )
+            ] + rows_to(first, count, start, down)
+
+        def side(first, count):
+            return rows_to(first, count, low + first, x)
+
+        rest = HALO - CHUNK
+        end_d, side_d = south(rows - CHUNK, CHUNK), side(rows - CHUNK, CHUNK)
+        end_a, side_a = north(0, CHUNK), side(0, CHUNK)
+        side_c = side(2 * CHUNK - 8, CHUNK + 8)
+        top_c = north(CHUNK, rest)
+        late_c = side(CHUNK, 8) + south(rows - HALO, rest)
+        side_b = side(HALO, CHUNK - 16)
+        parts = {
+            "d": end_d + side_d,
+            "a": end_a + side_a,
+            "c": side_c + top_c + late_c,
+            "b": side_b,
+        }
+        early = end_a + top_c + side_d + side_c
+        late = end_d + side_a + late_c + side_b
+        return parts, early, late
 
     def weights_pass(n):
         def body(i, _):
@@ -214,85 +239,142 @@
 
         lax.fori_loop(0, groups, body, 0)
 
-    def shift(src, n, k, sign):
-        a, b = sign * off[n, k, 0], sign * off[n, k, 1]
-        start = HALO + a - 1
+    def shift(src, dst, n, k, row0, sign):
+        a, b = sign * off[n, 0, k], sign * off[n, 1, k]
+        start = HALO + row0 + a - 1
         lane = lanes_of(PIECE)
+        held = {}
+
+        def turn(m, p, first, second, split, amount):
+            r = pl.ds(start + p, PIECE)
+            both = jnp.where(lane < split, src[first, r, :], src[second, r, :])
+            held[m, p] = pltpu.roll(both, amount, 1)
+
+        def put(m, p):
+            dst[k, m, p : p + PIECE, :] = held.pop((m, p))
+
+        turns, puts = [], []
         for m in range(taps):
             total = b + (m - 1)
             tile = lax.bitwise_and(total, tiles - 1)
             by = lax.shift_right_arithmetic(total, tiles.bit_length() - 1)
+            below = tiles * lax.shift_right_logical(by, 31)
+            split = lax.bitwise_and(by, LANES - 1)
             amount = lax.bitwise_and(-by, LANES - 1)
-            inside = lane - by
-            mine = jnp.logical_and(inside >= 0, inside < LANES)
-            for p in range(0, rows + 8, PIECE):
-                r = pl.ds(start + p, PIECE)
-                both = jnp.where(mine, src[tile, r, :], halo[tile, r, :])
-                moved[k, m, p : p + PIECE, :] = pltpu.roll(both, amount, 1)
-
-    def sample(w, k, c, j):
+            for p in range(0, GROWS, PIECE):
+                turns.append(functools.partial(turn, m, p, tile + tiles - below, tile + below, split, amount))
+                puts.append(functools.partial(put, m, p))
+        return turns, puts
+
+    def staggered(turns, puts, lag):
+        for at in range(len(turns) + lag):
+            now = []
+            if at < len(turns):
+                now.append(turns[at])
+            if at >= lag:
+                now.append(puts[at - lag])
+            yield now
+
+    def weave(main, side):
+        done = 0
+        for at, step in enumerate(main):
+            step()
+            due = (at + 1) * len(side) // len(main)
+            for i in range(done, due):
+                for one in side[i]:
+                    one()
+            done = due
+
+    def sample(src, w, k, c, j):
         acc = None
         for a in range(4):
             for b in range(4):
-                part = w[a * 4 + b] * moved[k, c + b, pl.ds(j + a, 8), :]
+                part = w[a * 4 + b] * src[k, c + b, pl.ds(j + a, 8), :]
                 acc = part if acc is None else acc + part
         return acc
 
-    def backward_rows(dst, n, g):
-        j = pl.multiple_of(g * 8, 8)
-        here = pl.ds(pl.multiple_of(HALO + j, 8), 8)
+    def backward_rows(src, dst, n, row0, i):
+        j = pl.multiple_of(i * 8, 8)
+        g = row0 // 8 + i
+        r = pl.ds(pl.multiple_of(row0 + j, 8), 8)
+        here = pl.ds(pl.multiple_of(HALO + row0 + j, 8), 8)
+        out = []
         for c in range(tiles):
-            w = [wts[c, g, m] for m in range(16)]
-            q = [sample(w, k, c, j) + time_step * cost[n, k] for k in range(controls)]
-            lowest = functools.reduce(jnp.minimum, q)
-            edge = lowest + temper
-            total = None
-            for k in range(controls):
-                ramp = jnp.maximum(edge - q[k], 0.0)
-                ramps[n, c, g, k] = ramp
-                total = ramp if total is None else total + ramp
-            recip[n, c, g] = 1.0 / total
-            dst[c, here, :] = lowest + time_step * cr[pl.ds(j, 8), pl.ds(c * LANES, LANES)]
-
-    def forward_rows(dst, n, g):
-        j = pl.multiple_of(g * 8, 8)
-        here = pl.ds(pl.multiple_of(HALO + j, 8), 8)
-        added = sums[n]
+            w, q = [], []
+
+            def take(k, c=c, w=w, q=q):
+                if k == 0:
+                    w.extend(wts[c, g, m] for m in range(16))
+                q.append(sample(src, w, k, c, j) + time_step * cost[n, k])
+                if k == controls - 1:
+                    lowest = functools.reduce(jnp.minimum, q)
+                    edge = lowest + temper
+                    total = None
+                    for kk in range(controls):
+                        ramp = jnp.maximum(edge - q[kk], 0.0)
+                        ramps[n, c, g, kk] = ramp
+                        total = ramp if total is None else total + ramp
+                    recip[n, c, g] = 1.0 / total
+                    dst[c, here, :] = lowest + time_step * cr[r, pl.ds(c * LANES, LANES)]
+
+            out += [functools.partial(take, k) for k in range(controls)]
+        return out
+
+    def forward_rows(src, dst, n, row0, i):
+        j = pl.multiple_of(i * 8, 8)
+        g = row0 // 8 + i
+        here = pl.ds(pl.multiple_of(HALO + row0 + j, 8), 8)
+        out, added = [], []
         for c in range(tiles):
-            w = [wts[c, g, m] for m in range(16)]
-            acc = None
-            for k in range(controls):
-                part = ramps[n, c, g, k] * sample(w, k, c, j)
-                acc = part if acc is None else acc + part
-            acc = jnp.maximum(acc * recip[n, c, g], 0.0)
-            dst[c, here, :] = acc
-            added = added + acc
-        sums[n] = added
-
-    def wait_all(buf, slot):
-        outer, inner = exchange(buf, slot)
-        for d in outer + inner:
-            d.wait()
+            w, acc = [], []
+
+            def take(k, c=c, w=w, acc=acc):
+                if k == 0:
+                    w.extend(wts[c, g, m] for m in range(16))
+                part = ramps[n, c, g, k] * sample(src, w, k, c, j)
+                acc.append(part if k == 0 else acc[-1] + part)
+                if k == controls - 1:
+                    arrived = jnp.maximum(acc[-1] * recip[n, c, g], 0.0)
+                    dst[c, here, :] = arrived
+                    added.append(arrived)
+                    if c == tiles - 1:
+                        sums[n] = sums[n] + functools.reduce(jnp.add, added)
+
+            out += [functools.partial(take, k) for k in range(controls)]
+        return out
+
+    per = CHUNK // 8
+    mine = {"d": rows - CHUNK, "a": 0, "c": 2 * CHUNK, "b": CHUNK}
 
     def stage(src, dst, slot_src, slot_dst, n, sign, rows_fn, send, fresh):
         if fresh:
             in_place(fr.at[n, 0])
             in_place(fr.at[n, 1])
         weights_pass(n)
-        wait_all(src, slot_src)
-        unpack(slot_src)
-
-        def shifts(k, _):
-            shift(src, n, k, sign)
+        _, early, late = exchange(src, slot_src)
+        for d in early:
+            d.wait()
+        unpack(src, slot_src, 2 * (low // 8) + 6, (high + HALO) // 8, 2)
+        take_end(src, slot_src, 1)
+
+        def first(k, _):
+            for now in staggered(*shift(src, ga, n, k, mine["d"], sign), 20):
+                for one in now:
+                    one()
             return 0
 
-        lax.fori_loop(0, controls, shifts, 0)
-        outer, inner = exchange(dst, slot_dst)
-
-        def publish(pack_fn, copies):
+        lax.fori_loop(0, controls, first, 0)
+        for d in late:
+            d.wait()
+        unpack(src, slot_src, 0, 2 * (low // 8) + 6, 3)
+        take_end(src, slot_src, 0)
+        parts, _, _ = exchange(dst, slot_dst)
+
+        def publish(name, pieces):
             def go():
-                pack_fn(dst, slot_dst)
-                for d in copies:
+                for at, count in pieces:
+                    pack(dst, slot_dst, at, count)
+                for d in parts[name]:
                     d.start()
 
             if send is True:
@@ -300,25 +382,36 @@
             else:
                 pl.when(send)(go)
 
-        def outer_rows(t, _):
-            rows_fn(dst, n, t + core * (t // rim))
-            return 0
-
-        def inner_rows(t, _):
-            rows_fn(dst, n, t + rim)
-            return 0
-
-        lax.fori_loop(0, 2 * rim, outer_rows, 0)
-        publish(pack_outer, outer)
-        lax.fori_loop(0, core, inner_rows, 0)
-        publish(pack_inner, inner)
+        def block(now, later, name, following, start, stop, shift_from, place):
+            def body(i, _):
+                side = []
+                if following is not None:
+                    side = list(staggered(*shift(src, later, n, i + shift_from, mine[following], sign), LAG))
+                weave(rows_fn(now, dst, n, mine[name], place(i)), side)
+                return 0
+
+            lax.fori_loop(start, stop, body, 0)
+
+        def plain(i):
+            return i
+
+        block(ga, gb, "d", "a", 0, per, 0, plain)
+        publish("d", [(mine["d"] // 8, per)])
+        block(gb, ga, "a", "c", 0, per, 0, plain)
+        publish("a", [(0, per)])
+        block(ga, gb, "c", "b", 0, per, 0, plain)
+        block(gb, None, "b", None, 0, 2, 0, lambda i: (per - 1) * (1 - i))
+        publish("c", [(mine["c"] // 8 - 1, per + 1), (per, 1)])
+        block(gb, None, "b", None, 1, per - 1, 0, plain)
+        publish("b", [(per + 1, per - 2)])
 
     def begin(load, src, buf, slot):
         load.wait()
         enter(src, buf)
-        pack_outer(buf, slot)
-        pack_inner(buf, slot)
-        return [d for part in exchange(buf, slot) for d in part]
+        for part in range(4):
+            pack(buf, slot, part * (groups // 4), groups // 4)
+        _, early, late = exchange(buf, slot)
+        return early + late
 
     first = begin(load_term, stage_a, ea, 0)
     pl.semaphore_wait(barrier, 8)
@@ -402,7 +495,6 @@
     nx, ny = lax.axis_size("gx"), lax.axis_size("gy")
     field = jax.ShapeDtypeStruct((rows, cols), jnp.float32)
     tall = rows + 2 * HALO
-    copies = 12
 
     def vmem(*shape):
         return pltpu.VMEM(shape, jnp.float32)
@@ -418,13 +510,14 @@
             vmem(steps, 8, LANES),
             vmem(ny, 8, LANES),
             vmem(nx, 8, LANES),
-            vmem(tiles, tall, LANES),
-            vmem(tiles, tall, LANES),
-            vmem(tiles, tall, LANES),
+            vmem(2 * tiles, tall, LANES),
+            vmem(2 * tiles, tall, LANES),
+            vmem(2 * tiles, tall, LANES),
+            vmem(3, 2, tiles, HALO, LANES),
             vmem(3, 2, tall, LANES),
             vmem(3, 2, rows, LANES),
-            vmem(tiles, tall, LANES),
-            vmem(controls, tiles + 3, rows + 8, LANES),
+            vmem(controls, tiles + 3, GROWS, LANES),
+            vmem(controls, tiles + 3, GROWS, LANES),
             vmem(tiles, rows // 8, 16, 8, LANES),
             vmem(steps, tiles, rows // 8, controls, 8, LANES),
             vmem(steps, tiles, rows // 8, 8, LANES),
@@ -434,15 +527,15 @@
             vmem(rows, cols),
             pltpu.VMEM((cols, cols), jnp.bfloat16),
             pltpu.SemaphoreType.DMA((3 + steps,)),
-            pltpu.SemaphoreType.DMA((3, copies)),
-            pltpu.SemaphoreType.DMA((3, copies)),
+            pltpu.SemaphoreType.DMA((3, COPIES)),
+            pltpu.SemaphoreType.DMA((3, COPIES)),
             pltpu.SemaphoreType.DMA((nx + ny,)),
             pltpu.SemaphoreType.DMA((nx + ny,)),
         ],
         compiler_params=pltpu.CompilerParams(
             collective_id=0, has_side_effects=True, vmem_limit_bytes=60 * 2**20
         ),
-    )(offsets, control_cost, terminal, crowding, density, fractions)
+    )(jnp.swapaxes(offsets, 1, 2), control_cost, terminal, crowding, density, fractions)
     return value, mass, masses[:steps, 0]
 
 

time: 157 us -> 142 us (0.904)
  Pallas kernels: 149 us -> 136 us
    pallas_call x1, Pallas kernels: 149 us -> 136 us  [shards(): pl.pallas_call(kernel, out_shape=(field, field, jax.ShapeDtypeStruct((8,...]
    unnamed x3 -> x2, local copies, waits for them, and re-layouts: 5.12 us -> 3.73 us
where the time goes in v3:
time: 142 us
  Pallas kernels  136 us (96%)
  local copies, waits for them, and re-layouts  5.04 us (4%)
    pallas_call x1, Pallas kernels, shards(): pl.pallas_call(kernel, out_shape=(field, field, jax.ShapeDtypeStruct((8,...  136 us
    unnamed x2, local copies, waits for them, and re-layouts  3.73 us

profile of v3, /device:TPU:1, one launch (start us, length us, event | category | flops | bytes accessed | tf_op | source)
XLA Modules:
  0.0 142.1 jit_solution(13584335378958175283)
XLA Ops:
  0.6 136.4 %shard_map.85 = (f32[256,512]{1,0:T(8,128)}, f32[256,512]{1,0:T(8,128)}, f32[8,128]{1,0:T(8,128)}) custom-call(s32[4,2,8]{2,1,0:T(2,128)} %bitcast.1, f32[4,8]{1,0:T(4,128)} %cost.1, f32[256,512]{1,0:T(8,128)} %term.1, f32[256,512]{1,0:T(8,128)} %crowd.1, f32[256,512]{1,0:T(8,128)} %dens.1, f32[4,2,256,512]{3,2,1,0:T(8,128)} %frac.1), custom_call_target="tpu_custom_call" | custom-call | tf_op jit(solution)/shard_map/pallas_call | solution.py:504
  137.0 1.3 slice_reduce_fusion
  138.3 1.9 %copy.11 = f32[256,512]{1,0:T(8,128)} copy(f32[256,512]{1,0:T(8,128)} %get-tuple-element.12) | data formatting | bytes 1048576
  140.2 1.9 %copy.12 = f32[256,512]{1,0:T(8,128)} copy(f32[256,512]{1,0:T(8,128)} %get-tuple-element.13) | data formatting | bytes 1048576

commit v4 on v3

--- a/solution.py
+++ b/solution.py
@@ -16,7 +16,7 @@
 GROWS = CHUNK + 8
 EDGE = 32
 LAG = 6
-COPIES = 22
+COPIES = 32
 
 time_step = 0.1
 temper = 0.3
@@ -34,7 +34,7 @@
 
 def kernel(
     off, cost, term, crowd, dens, frac,
-    value_out, mass_out, masses_out,
+    value_out, mass_out, totals_out,
     sums, part_y, part_x, ea, eb, ec, ends, strips, packs, ga, gb,
     wts, ramps, recip, cr, fr, stage_a, stage_b, order,
     load_sem, send_sem, recv_sem, sum_send, sum_recv,
@@ -112,12 +112,10 @@
 
         each_block(body)
 
-    def leave(buf, dst, factor):
+    def leave(buf, dst):
         def body(r):
             here = pl.ds(pl.multiple_of(HALO + r, 8), BLOCK)
             whole = jnp.concatenate([buf[c, here, :] for c in range(tiles)], axis=1)
-            if factor is not None:
-                whole = whole * factor
             dst[pl.ds(r, BLOCK), :] = reorder(whole, True)
 
         each_block(body)
@@ -208,21 +206,25 @@
         def side(first, count):
             return rows_to(first, count, low + first, x)
 
-        rest = HALO - CHUNK
-        end_d, side_d = south(rows - CHUNK, CHUNK), side(rows - CHUNK, CHUNK)
-        end_a, side_a = north(0, CHUNK), side(0, CHUNK)
+        rest, half = HALO - CHUNK, CHUNK // 2
+        end_d = [south(rows - CHUNK + part * half, half) for part in range(2)]
+        side_d = [side(rows - CHUNK + part * half, half) for part in range(2)]
+        end_a = [north(part * half, half) for part in range(2)]
+        side_a = [side(part * half, half) for part in range(2)]
         side_c = side(2 * CHUNK - 8, CHUNK + 8)
         top_c = north(CHUNK, rest)
         late_c = side(CHUNK, 8) + south(rows - HALO, rest)
         side_b = side(HALO, CHUNK - 16)
         parts = {
-            "d": end_d + side_d,
-            "a": end_a + side_a,
+            "d0": end_d[0] + side_d[0],
+            "d1": end_d[1] + side_d[1],
+            "a0": end_a[0] + side_a[0],
+            "a1": end_a[1] + side_a[1],
             "c": side_c + top_c + late_c,
             "b": side_b,
         }
-        early = end_a + top_c + side_d + side_c
-        late = end_d + side_a + late_c + side_b
+        early = end_a[0] + end_a[1] + top_c + side_d[0] + side_d[1] + side_c
+        late = end_d[0] + end_d[1] + side_a[0] + side_a[1] + late_c + side_b
         return parts, early, late
 
     def weights_pass(n):
@@ -358,36 +360,48 @@
         take_end(src, slot_src, 1)
 
         def first(k, _):
-            for now in staggered(*shift(src, ga, n, k, mine["d"], sign), 20):
-                for one in now:
-                    one()
+            one, two = (shift(src, ga, n, 2 * k + u, mine["d"], sign) for u in range(2))
+            for now in staggered(one[0] + two[0], one[1] + two[1], 20):
+                for step in now:
+                    step()
             return 0
 
-        lax.fori_loop(0, controls, first, 0)
+        lax.fori_loop(0, controls // 2, first, 0)
         for d in late:
             d.wait()
         unpack(src, slot_src, 0, 2 * (low // 8) + 6, 3)
         take_end(src, slot_src, 0)
         parts, _, _ = exchange(dst, slot_dst)
 
+        def put_out(name, pieces):
+            for at, count in pieces:
+                pack(dst, slot_dst, at, count)
+            for d in parts[name]:
+                d.start()
+
         def publish(name, pieces):
-            def go():
-                for at, count in pieces:
-                    pack(dst, slot_dst, at, count)
-                for d in parts[name]:
-                    d.start()
-
             if send is True:
-                go()
+                put_out(name, pieces)
             else:
-                pl.when(send)(go)
-
-        def block(now, later, name, following, start, stop, shift_from, place):
+                pl.when(send)(functools.partial(put_out, name, pieces))
+
+        def block(now, later, name, following, start, stop, place, halves=False):
             def body(i, _):
                 side = []
                 if following is not None:
-                    side = list(staggered(*shift(src, later, n, i + shift_from, mine[following], sign), LAG))
+                    side = list(staggered(*shift(src, later, n, i, mine[following], sign), LAG))
                 weave(rows_fn(now, dst, n, mine[name], place(i)), side)
+                if halves:
+                    for part in range(2):
+                        ready = i == (part + 1) * per // 2 - 1
+                        if send is not True:
+                            ready = jnp.logical_and(ready, send)
+                        at = mine[name] // 8 + part * (per // 2)
+
+                        @pl.when(ready)
+                        def _(part=part, at=at):
+                            put_out(f"{name}{part}", [(at, per // 2)])
+
                 return 0
 
             lax.fori_loop(start, stop, body, 0)
@@ -395,14 +409,12 @@
         def plain(i):
             return i
 
-        block(ga, gb, "d", "a", 0, per, 0, plain)
-        publish("d", [(mine["d"] // 8, per)])
-        block(gb, ga, "a", "c", 0, per, 0, plain)
-        publish("a", [(0, per)])
-        block(ga, gb, "c", "b", 0, per, 0, plain)
-        block(gb, None, "b", None, 0, 2, 0, lambda i: (per - 1) * (1 - i))
+        block(ga, gb, "d", "a", 0, per, plain, True)
+        block(gb, ga, "a", "c", 0, per, plain, True)
+        block(ga, gb, "c", "b", 0, per, plain)
+        block(gb, None, "b", None, 0, 2, lambda i: (per - 1) * (1 - i))
         publish("c", [(mine["c"] // 8 - 1, per + 1), (per, 1)])
-        block(gb, None, "b", None, 1, per - 1, 0, plain)
+        block(gb, None, "b", None, 1, per - 1, plain)
         publish("b", [(per + 1, per - 2)])
 
     def begin(load, src, buf, slot):
@@ -432,7 +444,7 @@
         return 0
 
     lax.fori_loop(0, steps // 2, backward_pair, 0)
-    leave(ea, stage_a, None)
+    leave(ea, stage_a)
     store_value = pltpu.make_async_copy(stage_a, value_out, load_sem.at[0])
     store_value.start()
 
@@ -459,33 +471,42 @@
             )
         for copy in copies:
             copy.start()
-        for copy in copies:
-            copy.wait()
-        total = part[0]
-        for hop in range(1, count):
-            total = total + part[hop]
-        return total
+
+        def finish():
+            for copy in copies:
+                copy.wait()
+            total = part[0]
+            for hop in range(1, count):
+                total = total + part[hop]
+            return total
+
+        return finish
 
     own = [jnp.sum(sums[n], axis=0, keepdims=True) for n in range(steps)]
     part_y[0] = jnp.concatenate(own + [jnp.zeros((8 - steps, LANES), jnp.float32)], axis=0)
-    part_x[0] = spread(part_y, ny, lambda j: (x, j), y, 0)
-    whole = spread(part_x, nx, lambda i: (i, y), x, ny)
-    totals = jnp.sum(whole, axis=1, keepdims=True) * (1.0 / (rows * cols * nx * ny))
-    scale = jnp.ones((1, 1), jnp.float32)
-    found = []
-    for n in range(steps):
-        mean = totals[n : n + 1, :] / scale
-        found.append(mean)
-        scale = scale * (mean + epsilon)
-    found.append(jnp.zeros((8 - steps, 1), jnp.float32))
-    masses_out[...] = jnp.broadcast_to(jnp.concatenate(found, axis=0), (8, LANES))
-    factor = jnp.broadcast_to(1.0 / scale, (BLOCK, cols))
-
-    leave(ec, stage_b, factor)
+    finish_y = spread(part_y, ny, lambda j: (x, j), y, 0)
+    leave(ec, stage_b)
     store_mass = pltpu.make_async_copy(stage_b, mass_out, load_sem.at[1])
     store_mass.start()
+    part_x[0] = finish_y()
+    finish_x = spread(part_x, nx, lambda i: (i, y), x, ny)
     store_mass.wait()
     store_value.wait()
+    whole = finish_x()
+    totals = jnp.sum(whole, axis=1, keepdims=True) * (1.0 / (rows * cols * nx * ny))
+    totals_out[...] = jnp.broadcast_to(totals, (8, LANES))
+
+
+def finish_kernel(value, mass, totals, value_out, mass_out, masses_out):
+    steps = masses_out.shape[0]
+    scale = jnp.float32(1.0)
+    for n in range(steps):
+        mean = totals[n, 0] / scale
+        masses_out[n] = mean
+        scale = scale * (mean + epsilon)
+    factor = 1.0 / jnp.full(mass.shape, scale, jnp.float32)
+    value_out[...] = value[...]
+    mass_out[...] = mass[...] * factor
 
 
 def shards(terminal, crowding, density, fractions, offsets, control_cost):
@@ -501,7 +522,7 @@
 
     smem = pl.BlockSpec(memory_space=pltpu.SMEM)
     hbm = pl.BlockSpec(memory_space=pl.ANY)
-    value, mass, masses = pl.pallas_call(
+    value, mass, totals = pl.pallas_call(
         kernel,
         out_shape=(field, field, jax.ShapeDtypeStruct((8, LANES), jnp.float32)),
         in_specs=[smem, smem, hbm, hbm, hbm, hbm],
@@ -536,7 +557,13 @@
             collective_id=0, has_side_effects=True, vmem_limit_bytes=60 * 2**20
         ),
     )(jnp.swapaxes(offsets, 1, 2), control_cost, terminal, crowding, density, fractions)
-    return value, mass, masses[:steps, 0]
+    whole = pl.BlockSpec(memory_space=pltpu.VMEM)
+    return pl.pallas_call(
+        finish_kernel,
+        out_shape=(field, field, jax.ShapeDtypeStruct((steps,), jnp.float32)),
+        in_specs=[whole, whole, smem],
+        out_specs=(whole, whole, smem),
+    )(value, mass, totals)
 
 
 def solution(mesh):

time: 142 us -> 139 us (0.979)
  local copies, waits for them, and re-layouts: 5.04 us -> 0 us
  Pallas kernels: 136 us -> 138 us
    unnamed x2 -> x0, local copies, waits for them, and re-layouts: 3.73 us -> none
    pallas_call x0 -> x1, Pallas kernels: none -> 2.24 us  [shards(): pl.pallas_call(finish_kernel, out_shape=(field, field, jax.ShapeDtypeStru...]
where the time goes in v4:
time: 139 us
  Pallas kernels  138 us (99%)
    pallas_call x1, Pallas kernels, shards(): pl.pallas_call(kernel, out_shape=(field, field, jax.ShapeDtypeStruct((8,...  136 us

profile of v4, /device:TPU:1, one launch (start us, length us, event | category | flops | bytes accessed | tf_op | source)
XLA Modules:
  0.0 139.1 jit_solution(7019352351279681655)
XLA Ops:
  0.6 136.2 %shard_map.85 = (f32[256,512]{1,0:T(8,128)}, f32[256,512]{1,0:T(8,128)}, f32[8,128]{1,0:T(8,128)}) custom-call(s32[4,2,8]{2,1,0:T(2,128)} %bitcast.1, f32[4,8]{1,0:T(4,128)} %cost.1, f32[256,512]{1,0:T(8,128)} %term.1, f32[256,512]{1,0:T(8,128)} %crowd.1, f32[256,512]{1,0:T(8,128)} %dens.1, f32[4,2,256,512]{3,2,1,0:T(8,128)} %frac.1), custom_call_target="tpu_custom_call" | custom-call | tf_op jit(solution)/shard_map/pallas_call | solution.py:525
  136.9 2.2 %shard_map.86 = (f32[256,512]{1,0:T(8,128)}, f32[256,512]{1,0:T(8,128)}, f32[4]{0:T(128)}) custom-call(f32[256,512]{1,0:T(8,128)} %get-tuple-element.6.value, f32[256,512]{1,0:T(8,128)} %get-tuple-element.7.mass, f32[8,128]{1,0:T(8,128)} %get-tuple-element.8.totals), custom_call_target="tpu_custom_call" | custom-call | tf_op jit(solution)/shard_map/pallas_call | solution.py:561

commit v5 on v4

--- a/solution.py
+++ b/solution.py
@@ -10,12 +10,12 @@
 MESH = pl.DeviceIdType.MESH
 LANES = 128
 HALO = 72
-PIECE = 24
+PIECE = 72
 BLOCK = 128
 CHUNK = 64
 GROWS = CHUNK + 8
 EDGE = 32
-LAG = 6
+LAG = 2
 COPIES = 32
 
 time_step = 0.1
@@ -160,7 +160,7 @@
         for c in range(tiles):
             buf[c, start : start + HALO, :] = ends[slot, side, c]
 
-    def exchange(buf, slot):
+    def exchange(buf, slot, down_last):
         index = iter(range(COPIES))
 
         def send(src, dst, i, j):
@@ -211,20 +211,29 @@
         side_d = [side(rows - CHUNK + part * half, half) for part in range(2)]
         end_a = [north(part * half, half) for part in range(2)]
         side_a = [side(part * half, half) for part in range(2)]
-        side_c = side(2 * CHUNK - 8, CHUNK + 8)
-        top_c = north(CHUNK, rest)
-        late_c = side(CHUNK, 8) + south(rows - HALO, rest)
-        side_b = side(HALO, CHUNK - 16)
+        if down_last:
+            first_m = side(CHUNK, CHUNK + 8) + south(rows - HALO, rest)
+            later_m = side(rows - HALO, rest) + north(CHUNK, rest)
+            side_z = side(2 * CHUNK + 8, CHUNK - 16)
+        else:
+            first_m = side(2 * CHUNK - 8, CHUNK + 8) + north(CHUNK, rest)
+            later_m = side(CHUNK, rest) + south(rows - HALO, rest)
+            side_z = side(HALO, CHUNK - 16)
         parts = {
             "d0": end_d[0] + side_d[0],
             "d1": end_d[1] + side_d[1],
             "a0": end_a[0] + side_a[0],
             "a1": end_a[1] + side_a[1],
-            "c": side_c + top_c + late_c,
-            "b": side_b,
+            "m": first_m + later_m,
+            "z": side_z,
         }
-        early = end_a[0] + end_a[1] + top_c + side_d[0] + side_d[1] + side_c
-        late = end_d[0] + end_d[1] + side_a[0] + side_a[1] + late_c + side_b
+        ends_d, ends_a = end_d[0] + end_d[1], end_a[0] + end_a[1]
+        sides_d, sides_a = side_d[0] + side_d[1], side_a[0] + side_a[1]
+        if down_last:
+            early, late = ends_d + sides_a, ends_a + sides_d
+        else:
+            early, late = ends_a + sides_d, ends_d + sides_a
+        early, late = early + first_m, late + later_m + side_z
         return parts, early, late
 
     def weights_pass(n):
@@ -328,15 +337,18 @@
         here = pl.ds(pl.multiple_of(HALO + row0 + j, 8), 8)
         out, added = [], []
         for c in range(tiles):
-            w, acc = [], []
-
-            def take(k, c=c, w=w, acc=acc):
+            w, q = [], []
+
+            def take(k, c=c, w=w, q=q):
                 if k == 0:
                     w.extend(wts[c, g, m] for m in range(16))
-                part = ramps[n, c, g, k] * sample(src, w, k, c, j)
-                acc.append(part if k == 0 else acc[-1] + part)
+                q.append(sample(src, w, k, c, j))
                 if k == controls - 1:
-                    arrived = jnp.maximum(acc[-1] * recip[n, c, g], 0.0)
+                    acc = None
+                    for kk in range(controls):
+                        part = ramps[n, c, g, kk] * q[kk]
+                        acc = part if acc is None else acc + part
+                    arrived = jnp.maximum(acc * recip[n, c, g], 0.0)
                     dst[c, here, :] = arrived
                     added.append(arrived)
                     if c == tiles - 1:
@@ -348,19 +360,23 @@
     per = CHUNK // 8
     mine = {"d": rows - CHUNK, "a": 0, "c": 2 * CHUNK, "b": CHUNK}
 
-    def stage(src, dst, slot_src, slot_dst, n, sign, rows_fn, send, fresh):
+    def stage(src, dst, slot_src, slot_dst, n, sign, rows_fn, send, fresh, d_first):
         if fresh:
             in_place(fr.at[n, 0])
             in_place(fr.at[n, 1])
         weights_pass(n)
-        _, early, late = exchange(src, slot_src)
+        _, early, late = exchange(src, slot_src, not d_first)
         for d in early:
             d.wait()
-        unpack(src, slot_src, 2 * (low // 8) + 6, (high + HALO) // 8, 2)
-        take_end(src, slot_src, 1)
+        all_rows, cut = (high + HALO) // 8, 13 * 2
+        if d_first:
+            unpack(src, slot_src, all_rows - cut, all_rows, 2)
+        else:
+            unpack(src, slot_src, 0, cut, 2)
+        take_end(src, slot_src, 1 if d_first else 0)
 
         def first(k, _):
-            one, two = (shift(src, ga, n, 2 * k + u, mine["d"], sign) for u in range(2))
+            one, two = (shift(src, ga, n, 2 * k + u, mine["d" if d_first else "a"], sign) for u in range(2))
             for now in staggered(one[0] + two[0], one[1] + two[1], 20):
                 for step in now:
                     step()
@@ -369,9 +385,12 @@
         lax.fori_loop(0, controls // 2, first, 0)
         for d in late:
             d.wait()
-        unpack(src, slot_src, 0, 2 * (low // 8) + 6, 3)
-        take_end(src, slot_src, 0)
-        parts, _, _ = exchange(dst, slot_dst)
+        if d_first:
+            unpack(src, slot_src, 0, all_rows - cut, 3)
+        else:
+            unpack(src, slot_src, cut, all_rows, 3)
+        take_end(src, slot_src, 0 if d_first else 1)
+        parts, _, _ = exchange(dst, slot_dst, d_first)
 
         def put_out(name, pieces):
             for at, count in pieces:
@@ -409,20 +428,25 @@
         def plain(i):
             return i
 
-        block(ga, gb, "d", "a", 0, per, plain, True)
-        block(gb, ga, "a", "c", 0, per, plain, True)
-        block(ga, gb, "c", "b", 0, per, plain)
-        block(gb, None, "b", None, 0, 2, lambda i: (per - 1) * (1 - i))
-        publish("c", [(mine["c"] // 8 - 1, per + 1), (per, 1)])
-        block(gb, None, "b", None, 1, per - 1, plain)
-        publish("b", [(per + 1, per - 2)])
+        turn = "dabc" if d_first else "adcb"
+        block(ga, gb, turn[0], turn[1], 0, per, plain, True)
+        block(gb, ga, turn[1], turn[2], 0, per, plain, True)
+        block(ga, gb, turn[2], turn[3], 0, per, plain)
+        block(gb, None, turn[3], None, 0, 2, lambda i: (per - 1) * (1 - i))
+        last = mine[turn[3]] // 8
+        if d_first:
+            publish("m", [(per, per + 1), (last + per - 1, 1)])
+        else:
+            publish("m", [(mine["c"] // 8 - 1, per + 1), (last, 1)])
+        block(gb, None, turn[3], None, 1, per - 1, plain)
+        publish("z", [(last + 1, per - 2)])
 
     def begin(load, src, buf, slot):
         load.wait()
         enter(src, buf)
         for part in range(4):
             pack(buf, slot, part * (groups // 4), groups // 4)
-        _, early, late = exchange(buf, slot)
+        _, early, late = exchange(buf, slot, False)
         return early + late
 
     first = begin(load_term, stage_a, ea, 0)
@@ -439,8 +463,8 @@
 
     def backward_pair(m, _):
         n = steps - 1 - 2 * m
-        stage(ea, eb, 0, 1, n, 1, backward_rows, True, True)
-        stage(eb, ea, 1, 0, n - 1, 1, backward_rows, m + 1 < steps // 2, True)
+        stage(ea, eb, 0, 1, n, 1, backward_rows, True, True, True)
+        stage(eb, ea, 1, 0, n - 1, 1, backward_rows, m + 1 < steps // 2, True, False)
         return 0
 
     lax.fori_loop(0, steps // 2, backward_pair, 0)
@@ -450,8 +474,8 @@
 
     def forward_pair(m, _):
         n = 2 * m
-        stage(ec, ea, 2, 0, n, -1, forward_rows, True, False)
-        stage(ea, ec, 0, 2, n + 1, -1, forward_rows, m + 1 < steps // 2, False)
+        stage(ec, ea, 2, 0, n, -1, forward_rows, True, False, True)
+        stage(ea, ec, 0, 2, n + 1, -1, forward_rows, m + 1 < steps // 2, False, False)
         return 0
 
     lax.fori_loop(0, steps // 2, forward_pair, 0)

time: 139 us -> 140 us (level)
  no operation moved by 1% of the time
where the time goes in v5:
time: 140 us
  Pallas kernels  139 us (99%)
    pallas_call x1, Pallas kernels, shards(): pl.pallas_call(kernel, out_shape=(field, field, jax.ShapeDtypeStruct((8,...  137 us

profile of v5, /device:TPU:1, one launch (start us, length us, event | category | flops | bytes accessed | tf_op | source)
XLA Modules:
  0.0 140.1 jit_solution(4032217465039381027)
XLA Ops:
  0.6 137.2 %shard_map.85 = (f32[256,512]{1,0:T(8,128)}, f32[256,512]{1,0:T(8,128)}, f32[8,128]{1,0:T(8,128)}) custom-call(s32[4,2,8]{2,1,0:T(2,128)} %bitcast.1, f32[4,8]{1,0:T(4,128)} %cost.1, f32[256,512]{1,0:T(8,128)} %term.1, f32[256,512]{1,0:T(8,128)} %crowd.1, f32[256,512]{1,0:T(8,128)} %dens.1, f32[4,2,256,512]{3,2,1,0:T(8,128)} %frac.1), custom_call_target="tpu_custom_call" | custom-call | tf_op jit(solution)/shard_map/pallas_call | solution.py:549
  137.9 2.2 %shard_map.86 = (f32[256,512]{1,0:T(8,128)}, f32[256,512]{1,0:T(8,128)}, f32[4]{0:T(128)}) custom-call(f32[256,512]{1,0:T(8,128)} %get-tuple-element.6.value, f32[256,512]{1,0:T(8,128)} %get-tuple-element.7.mass, f32[8,128]{1,0:T(8,128)} %get-tuple-element.8.totals), custom_call_target="tpu_custom_call" | custom-call | tf_op jit(solution)/shard_map/pallas_call | solution.py:585

commit v6 on v4

--- a/solution.py
+++ b/solution.py
@@ -10,12 +10,12 @@
 MESH = pl.DeviceIdType.MESH
 LANES = 128
 HALO = 72
-PIECE = 24
+PIECE = 72
 BLOCK = 128
 CHUNK = 64
 GROWS = CHUNK + 8
 EDGE = 32
-LAG = 6
+LAG = 2
 COPIES = 32
 
 time_step = 0.1
@@ -328,15 +328,18 @@
         here = pl.ds(pl.multiple_of(HALO + row0 + j, 8), 8)
         out, added = [], []
         for c in range(tiles):
-            w, acc = [], []
-
-            def take(k, c=c, w=w, acc=acc):
+            w, q = [], []
+
+            def take(k, c=c, w=w, q=q):
                 if k == 0:
                     w.extend(wts[c, g, m] for m in range(16))
-                part = ramps[n, c, g, k] * sample(src, w, k, c, j)
-                acc.append(part if k == 0 else acc[-1] + part)
+                q.append(sample(src, w, k, c, j))
                 if k == controls - 1:
-                    arrived = jnp.maximum(acc[-1] * recip[n, c, g], 0.0)
+                    acc = None
+                    for kk in range(controls):
+                        part = ramps[n, c, g, kk] * q[kk]
+                        acc = part if acc is None else acc + part
+                    arrived = jnp.maximum(acc * recip[n, c, g], 0.0)
                     dst[c, here, :] = arrived
                     added.append(arrived)
                     if c == tiles - 1:

time: 139 us -> 139 us (level)
  no operation moved by 1% of the time
where the time goes in v6:
time: 139 us; the launch traced here: 138 us
  Pallas kernels  138 us (99%)
    pallas_call x1, Pallas kernels, shards(): pl.pallas_call(kernel, out_shape=(field, field, jax.ShapeDtypeStruct((8,...  136 us

profile of v6, /device:TPU:1, one launch (start us, length us, event | category | flops | bytes accessed | tf_op | source)
XLA Modules:
  0.0 138.5 jit_solution(12130414166045851046)
XLA Ops:
  0.6 135.6 %shard_map.85 = (f32[256,512]{1,0:T(8,128)}, f32[256,512]{1,0:T(8,128)}, f32[8,128]{1,0:T(8,128)}) custom-call(s32[4,2,8]{2,1,0:T(2,128)} %bitcast.1, f32[4,8]{1,0:T(4,128)} %cost.1, f32[256,512]{1,0:T(8,128)} %term.1, f32[256,512]{1,0:T(8,128)} %crowd.1, f32[256,512]{1,0:T(8,128)} %dens.1, f32[4,2,256,512]{3,2,1,0:T(8,128)} %frac.1), custom_call_target="tpu_custom_call" | custom-call | tf_op jit(solution)/shard_map/pallas_call | solution.py:528
  136.2 2.2 %shard_map.86 = (f32[256,512]{1,0:T(8,128)}, f32[256,512]{1,0:T(8,128)}, f32[4]{0:T(128)}) custom-call(f32[256,512]{1,0:T(8,128)} %get-tuple-element.6.value, f32[256,512]{1,0:T(8,128)} %get-tuple-element.7.mass, f32[8,128]{1,0:T(8,128)} %get-tuple-element.8.totals), custom_call_target="tpu_custom_call" | custom-call | tf_op jit(solution)/shard_map/pallas_call | solution.py:564
